TPU v7x, 32 devices: a whole 2x2x4 slice. The times are simulated.
32 devices in a mesh: kpt: 16 (over z, y, x), aux: 2 (over core).
Axes of the slice: x: 2, y: 2, z: 4, core: 2. Of those that a mesh axis runs over, the one named last changes fastest.
Arguments:
- pair_tensors: bfloat16 [2, 32, 4, 512, 1024], P(None, 'kpt', 'aux'), may hold values from -0.1875 to 0.1875
- orbitals: bfloat16 [32, 512, 512], P('kpt'), may hold values from -6 to 6
- matchings: int32 [2, 32], replicated, may hold values from 0 to 31, as said below
Outputs:
- exchange: float32 [32, 2, 512, 512], P('kpt', None, 'aux')
Inputs may be any that keep to these rules, and one draw needn't show every extreme that they name: Each row matchings[r] is a permutation of the 32 k-points. With 2^m = 16 blocks of 2 consecutive k-points, round r matches every k-point of block d with a k-point of block d XOR 2^(m - 1 - r).
All inputs are finite; a program needn't handle non-finite values.
Results may differ from a plain program's by a relative error of at most 0.00098.
Values may be sent and summed in bfloat16 or wider, within the bound.
No kernel may reach another device: no remote copies, remote signals or barrier semaphores. Data moves between devices by JAX's collectives and lax.ppermute only.
A program may use at most 192 MiB of HBM per device.

v0:
```python
import jax
import jax.numpy as jnp
from jax import lax
from jax.sharding import PartitionSpec as P

ROUNDS = 2


def from_partner(shard, axis, distance):
    return lax.ppermute(shard, axis, [(i, i ^ 1 << distance) for i in range(lax.axis_size(axis))])


def build_block(chosen):
    occupied = chosen.shape[-1] // 2
    real_part = chosen[..., :occupied]
    imag_part = chosen[..., occupied:]
    upper_rows = jnp.concatenate([real_part, imag_part], axis=-1)
    bottom = jnp.concatenate([-imag_part, real_part], axis=-1)
    return jnp.concatenate([upper_rows, bottom], axis=-2)


def half_transform(pairs, block):
    return jnp.einsum("kpab,kbc->kpac", pairs, block, preferred_element_type=jnp.float32).astype(
        jnp.bfloat16
    )


def hermitian_rows(left_rows, half_done):
    occupied = half_done.shape[-1] // 2
    rotated = jnp.concatenate([-half_done[..., occupied:], half_done[..., :occupied]], axis=-1)
    exch_real = jnp.einsum(
        "kpac,kpbc->kab", left_rows, half_done, preferred_element_type=jnp.float32
    )
    exch_imag = jnp.einsum("kpac,kpbc->kab", left_rows, rotated, preferred_element_type=jnp.float32)
    return jnp.stack([exch_real, exch_imag], axis=1)


def body(pair_tensors, orbitals, matchings):
    per_device = orbitals.shape[0]
    occupied = orbitals.shape[2] // 2
    bit_count = lax.axis_size("kpt").bit_length() - 1
    factor = 1.0 / (ROUNDS * pair_tensors.shape[2] * lax.axis_size("aux") * occupied) ** 0.5
    offset = lax.axis_index("kpt") * per_device
    collected = []
    for which_round in range(ROUNDS):
        swap_bit = bit_count - 1 - which_round
        stride = orbitals.shape[2] // lax.axis_size("aux")
        piece = lax.dynamic_slice_in_dim(orbitals, lax.axis_index("aux") * stride, stride, 2)
        arrived = from_partner(piece, "kpt", swap_bit)
        partner = lax.all_gather(arrived, "aux", axis=2, tiled=True)
        within = lax.dynamic_slice_in_dim(matchings[which_round], offset, per_device) % per_device
        chosen = jnp.take(partner, within, axis=0)
        half_done = half_transform(pair_tensors[which_round], build_block(chosen))
        pieces = hermitian_rows(half_done, half_done) * factor
        collected.append(pieces)
    running = collected[0]
    for extra in collected[1:]:
        running = running + extra
    running = lax.psum_scatter(running, "aux", scatter_dimension=2, tiled=True)
    return running


def solution(mesh):
    placed = (P(None, "kpt", "aux", None, None), P("kpt", None, None), P())
    return jax.shard_map(
        body, mesh=mesh, in_specs=placed, out_specs=P("kpt", None, "aux", None), check_vma=False
    )
```

profile of v0, /device:TPU:0, one launch (start us, length us, event | category | flops | bytes accessed | tf_op | source)
XLA Modules:
  0.0 101.2 jit_solution(11582765281406286201)
XLA Ops:
  6.5 1.2 %copy-done = bf16[2,512,512]{2,1,0:T(8,128)(2,1)S(1)} copy-done((bf16[2,512,512]{2,1,0:T(8,128)(2,1)S(1)}, bf16[2,512,512]{2,1,0:T(8,128)(2,1)}, u32[]{:S(2)}) %copy-start) | copy-done | bytes 1048600
  7.8 3.1 %collective-permute-start.1 = (bf16[2,512,256]{2,1,0:T(8,128)(2,1)S(1)}, bf16[2,512,256]{2,1,0:T(8,128)(2,1)S(1)}, u32[]{:S(2)}, u32[]{:S(2)}) collective-permute-start(bf16[2,512,256]{2,1,0:T(8,128)(2,1)S(1)} %constant_dynamic-slice_fusion.2), channel_id=1, source_target_pairs={{0,8},{2,10},{4,12},{6,14},{8,0},{10,2},{12,4},{14,6},{16,24},{18,... | collective-permute-start | bytes 1572872 | tf_op jit(solution)/shard_map/ppermute | solution.py:10
  10.9 11.9 %collective-permute-done.1 = bf16[2,512,256]{2,1,0:T(8,128)(2,1)S(1)} collective-permute-done((bf16[2,512,256]{2,1,0:T(8,128)(2,1)S(1)}, bf16[2,512,256]{2,1,0:T(8,128)(2,1)S(1)}, u32[]{:S(2)}, u32[]{:S(2)}) %collective-permute-start.1) | collective-permute-done | bytes 524320 | tf_op jit(solution)/shard_map/ppermute | solution.py:10
  22.8 0.8 copy-done.7
  23.7 2.8 %collective-permute-start = (bf16[2,512,256]{2,1,0:T(8,128)(2,1)S(1)}, bf16[2,512,256]{2,1,0:T(8,128)(2,1)S(1)}, u32[]{:S(2)}, u32[]{:S(2)}) collective-permute-start(bf16[2,512,256]{2,1,0:T(8,128)(2,1)S(1)} %constant_dynamic-slice_fusion.2), channel_id=1, source_target_pairs={{0,16},{2,18},{4,20},{6,22},{8,24},{10,26},{12,28},{14,30},{16,0},... | collective-permute-start | bytes 1572872 | tf_op jit(solution)/shard_map/ppermute | solution.py:10
  26.5 0.8 fusion.41
  27.5 21.5 %collective-permute-done = bf16[2,512,256]{2,1,0:T(8,128)(2,1)S(1)} collective-permute-done((bf16[2,512,256]{2,1,0:T(8,128)(2,1)S(1)}, bf16[2,512,256]{2,1,0:T(8,128)(2,1)S(1)}, u32[]{:S(2)}, u32[]{:S(2)}) %collective-permute-start) | collective-permute-done | bytes 524320 | tf_op jit(solution)/shard_map/ppermute | solution.py:10
  49.0 0.8 copy-done.6
  49.9 1.8 %gather_fusion.1 = bf16[2,512,512]{2,1,0:T(8,128)(2,1)S(1)} fusion(bf16[2,512,512]{2,1,0:T(8,128)(2,1)} %all-gather.5.cloned.1.call-done, s32[1024]{0:T(1024)S(1)} %pad_clamp_fusion), kind=kCustom, calls=%fused_computation.1.clone | custom fusion | bytes 2097160 | tf_op jit(solution)/shard_map/jit(_take)/gather | solution.py:52
  51.7 0.5 copy.18
  52.5 4.6 %convert_bitcast_fusion = bf16[2,2,512,512]{2,3,1,0:T(8,128)(2,1)S(1)} fusion(bf16[2,2,2,512,1024]{4,3,2,1,0:T(8,128)(2,1)} %param.5, bf16[2,512,256]{1,2,0:T(8,128)(2,1)S(1)} %get-tuple-element.15, bf16[2,512,256]{1,2,0:T(8,128)(2,1)S(1)} %get-tuple-element.14, bf16[2,512,512]{1,2,0:T(8,128)(2,1)S(1)} %broadcast_select_fusion), kind=kOutput, calls=%fused_computation.28 | convolution fusion | flops 2154823680 | bytes 8388608 | tf_op jit(solution)/shard_map/kpab,kbc->kpac/dot_general | solution.py:23
  57.2 1.6 %slice_negate_fusion = (bf16[2,2,512,256]{2,3,1,0:T(8,128)(2,1)}, bf16[2,2,512,256]{2,3,1,0:T(8,128)(2,1)}) fusion(bf16[2,2,512,512]{2,3,1,0:T(8,128)(2,1)S(1)} %convert_bitcast_fusion), kind=kLoop, calls=%fused_computation.34 | loop fusion | flops 524288 | bytes 4194304 | tf_op jit(solution)/shard_map/neg | solution.py:30
  58.8 0.4 copy-done.1
  59.2 2.6 %convolution_bitcast_fusion = f32[2,1,512,512]{3,2,0,1:T(8,128)} fusion(bf16[2,2,512,512]{2,3,1,0:T(8,128)(2,1)S(1)} %convert_bitcast_fusion), kind=kOutput, calls=%fused_computation.32 | convolution fusion | flops 1073741824 | bytes 4194304 | tf_op jit(solution)/shard_map/kpac,kpbc->kab/dot_general | solution.py:31
  61.8 1.8 %gather_fusion = bf16[2,512,512]{2,1,0:T(8,128)(2,1)S(1)} fusion(bf16[2,512,512]{2,1,0:T(8,128)(2,1)} %all-gather.3.cloned.1.call-done, s32[1024]{0:T(1024)S(1)} %pad_clamp_fusion.1), kind=kCustom, calls=%fused_computation.clone | custom fusion | bytes 2097160 | tf_op jit(solution)/shard_map/jit(_take)/gather | solution.py:52
  63.6 0.5 copy.13
  64.4 4.6 %convert_bitcast_fusion.1 = bf16[2,2,512,512]{2,3,1,0:T(8,128)(2,1)S(1)} fusion(bf16[2,2,2,512,1024]{4,3,2,1,0:T(8,128)(2,1)} %param.5, bf16[2,512,256]{1,2,0:T(8,128)(2,1)S(1)} %get-tuple-element.17, bf16[2,512,256]{1,2,0:T(8,128)(2,1)S(1)} %get-tuple-element.16, bf16[2,512,512]{1,2,0:T(8,128)(2,1)S(1)} %broadcast_select_fusion.1), kind=kOutput, calls=%fused_computation.29 | convolution fusion | flops 2154823680 | bytes 8388608 | tf_op jit(solution)/shard_map/kpab,kbc->kpac/dot_general | solution.py:23
  69.0 1.3 %convolution_bitcast_fusion.1 = f32[2,1,512,512]{3,2,0,1:T(8,128)S(1)} fusion(bf16[2,2,512,512]{2,3,1,0:T(8,128)(2,1)S(1)} %convert_bitcast_fusion.1), kind=kOutput, calls=%fused_computation.33 | convolution fusion | flops 1073741824 | bytes 4194304 | tf_op jit(solution)/shard_map/kpac,kpbc->kab/dot_general | solution.py:31
  70.5 1.4 %copy-done.2 = bf16[2,2,512,512]{2,3,1,0:T(8,128)(2,1)S(1)} copy-done((bf16[2,2,512,512]{2,3,1,0:T(8,128)(2,1)S(1)}, bf16[2,2,512,512]{2,3,1,0:T(8,128)(2,1)}, u32[]{:S(2)}) %copy-start.2) | copy-done | bytes 2097176
  72.5 1.3 %fusion.27 = f32[2,1,512,512]{3,2,0,1:T(8,128)S(1)} fusion(bf16[2,2,512,512]{2,3,1,0:T(8,128)(2,1)S(1)} %copy-done.2, bf16[2,2,512,256]{2,3,1,0:T(8,128)(2,1)S(1)} %copy-done.5, bf16[2,2,512,256]{2,3,1,0:T(8,128)(2,1)S(1)} %copy-done.4), kind=kOutput, calls=%fused_computation.30 | convolution fusion | flops 1077936128 | bytes 6291456 | tf_op jit(solution)/shard_map/kpac,kpbc->kab/dot_general | solution.py:34
  73.8 1.3 %fusion.30 = f32[2,1,512,512]{3,2,0,1:T(8,128)S(1)} fusion(bf16[2,2,512,512]{2,3,1,0:T(8,128)(2,1)S(1)} %convert_bitcast_fusion.1, bf16[2,2,512,256]{2,3,1,0:T(8,128)(2,1)S(1)} %get-tuple-element.13, bf16[2,2,512,256]{2,3,1,0:T(8,128)(2,1)S(1)} %get-tuple-element.12), kind=kOutput, calls=%fused_computation.31 | convolution fusion | flops 1077936128 | bytes 6291456 | tf_op jit(solution)/shard_map/kpac,kpbc->kab/dot_general | solution.py:34
  75.4 3.0 %fusion = f32[2,2,512,512]{3,2,0,1:T(8,128)} fusion(f32[2,1,512,512]{3,2,0,1:T(8,128)S(1)} %fusion.30, f32[2,1,512,512]{3,2,0,1:T(8,128)S(1)} %convolution_bitcast_fusion.1, f32[2,1,512,512]{3,2,0,1:T(8,128)S(1)} %fusion.27, f32[2,1,512,512]{3,2,0,1:T(8,128)S(1)} %copy-done.3), kind=kLoop, calls=%fused_computation.3 | loop fusion | flops 4194304 | bytes 12582912 | tf_op jit(solution)/shard_map/add | solution.py:58
  78.4 13.2 %reduce-scatter.2.cloned.1.call-done = f32[2,2,256,512]{3,2,0,1:T(8,128)} async-done(((f32[2,2,512,512]{3,2,0,1:T(8,128)}), f32[2,2,256,512]{3,2,0,1:T(8,128)}) %reduce-scatter.2.cloned.1.call-update) | async-done | bytes 2097168 | tf_op jit(solution)/shard_map/reduce_scatter | solution.py:59
  91.6 3.1 %copy.23 = f32[2,2,256,512]{3,2,1,0:T(8,128)} copy(f32[2,2,256,512]{3,2,0,1:T(8,128)} %reduce-scatter.2.cloned.1.call-done) | data formatting | bytes 4194304 | tf_op jit(solution)/shard_map/reduce_scatter | solution.py:59
  (29 shorter events, 1.9 us)
Async XLA Ops:
  6.5 1.2 %copy-start = (bf16[2,512,512]{2,1,0:T(8,128)(2,1)S(1)}, bf16[2,512,512]{2,1,0:T(8,128)(2,1)}, u32[]{:S(2)}) copy-start(bf16[2,512,512]{2,1,0:T(8,128)(2,1)} %param.6) | copy-start | bytes 3145732
  6.5 43.3 %all-gather.5.cloned.1.call-start = ((), (), s32[]{:S(2)}) async-start(), calls=%async_computation.2 | async-start | bytes 1572864 | tf_op jit(solution)/shard_map/all_gather | solution.py:50
  7.8 15.0 %collective-permute-start.1 = (bf16[2,512,256]{2,1,0:T(8,128)(2,1)S(1)}, bf16[2,512,256]{2,1,0:T(8,128)(2,1)S(1)}, u32[]{:S(2)}, u32[]{:S(2)}) collective-permute-start(bf16[2,512,256]{2,1,0:T(8,128)(2,1)S(1)} %constant_dynamic-slice_fusion.2), channel_id=1, source_target_pairs={{0,8},{2,10},{4,12},{6,14},{8,0},{10,2},{12,4},{14,6},{16,24},{18,... | collective-permute-start | bytes 1572872 | tf_op jit(solution)/shard_map/ppermute | solution.py:10
  22.8 0.8 copy-start.7
  23.7 38.1 %all-gather.3.cloned.1.call-start = ((), (), s32[]{:S(2)}) async-start(), calls=%async_computation.1 | async-start | bytes 1572864 | tf_op jit(solution)/shard_map/all_gather | solution.py:50
  23.7 25.3 %collective-permute-start = (bf16[2,512,256]{2,1,0:T(8,128)(2,1)S(1)}, bf16[2,512,256]{2,1,0:T(8,128)(2,1)S(1)}, u32[]{:S(2)}, u32[]{:S(2)}) collective-permute-start(bf16[2,512,256]{2,1,0:T(8,128)(2,1)S(1)} %constant_dynamic-slice_fusion.2), channel_id=1, source_target_pairs={{0,16},{2,18},{4,20},{6,22},{8,24},{10,26},{12,28},{14,30},{16,0},... | collective-permute-start | bytes 1572872 | tf_op jit(solution)/shard_map/ppermute | solution.py:10
  49.0 0.8 copy-start.6
  49.8 41.7 %reduce-scatter.2.cloned.1.call-start = ((), (), s32[]{:S(2)}) async-start(), calls=%async_computation.3 | async-start | bytes 6291456 | tf_op jit(solution)/shard_map/reduce_scatter | solution.py:59
  57.1 2.0 %copy-start.1 = (bf16[2,2,512,512]{2,3,1,0:T(8,128)(2,1)}, bf16[2,2,512,512]{2,3,1,0:T(8,128)(2,1)S(1)}, u32[]{:S(2)}) copy-start(bf16[2,2,512,512]{2,3,1,0:T(8,128)(2,1)S(1)} %convert_bitcast_fusion) | copy-start | bytes 6291460
  70.3 1.6 %copy-start.2 = (bf16[2,2,512,512]{2,3,1,0:T(8,128)(2,1)S(1)}, bf16[2,2,512,512]{2,3,1,0:T(8,128)(2,1)}, u32[]{:S(2)}) copy-start(bf16[2,2,512,512]{2,3,1,0:T(8,128)(2,1)} %copy-done.1) | copy-start | bytes 6291460
  70.3 1.8 %copy-start.4 = (bf16[2,2,512,256]{2,3,1,0:T(8,128)(2,1)S(1)}, bf16[2,2,512,256]{2,3,1,0:T(8,128)(2,1)}, u32[]{:S(2)}) copy-start(bf16[2,2,512,256]{2,3,1,0:T(8,128)(2,1)} %get-tuple-element.10) | copy-start | bytes 3145732
  70.3 2.2 %copy-start.5 = (bf16[2,2,512,256]{2,3,1,0:T(8,128)(2,1)S(1)}, bf16[2,2,512,256]{2,3,1,0:T(8,128)(2,1)}, u32[]{:S(2)}) copy-start(bf16[2,2,512,256]{2,3,1,0:T(8,128)(2,1)} %get-tuple-element.11) | copy-start | bytes 3145732
  73.8 1.6 %copy-start.3 = (f32[2,1,512,512]{3,2,0,1:T(8,128)S(1)}, f32[2,1,512,512]{3,2,0,1:T(8,128)}, u32[]{:S(2)}) copy-start(f32[2,1,512,512]{3,2,0,1:T(8,128)} %convolution_bitcast_fusion) | copy-start | bytes 6291460
Sparse Core Ops, SparseCore 0:
  23.8 10.1 all-gather.4
  49.9 9.7 all-gather.2
  78.5 13.0 reduce-scatter.1
where the time goes:
time: 102 us; the launch traced here: 101 us
  waiting for transfers between devices  46.7 us (46%)
  matrix products  15.7 us (15%)
  local copies, waits for them, and re-layouts  14.1 us (14%)
  between operations  13.3 us (13%)
  starting transfers between devices  6.02 us (6%)
  other arithmetic  5.37 us (5%)
    ppermute x2, waiting for transfers between devices, from_partner(): lax.ppermute(shard, axis, [(i, i ^ 1 << distance) for i in range(lax.axis...  33.4 us
    reduce_scatter x1, waiting for transfers between devices, body(): running = lax.psum_scatter(running, 'aux', scatter_dimension=2, tiled=True)  13.2 us
    dot_general x2, matrix products, half_transform(): jnp.einsum('kpab,kbc->kpac', pairs, block, preferred_element_type=jnp.flo...  9.16 us
    ppermute x2, starting transfers between devices, from_partner(): lax.ppermute(shard, axis, [(i, i ^ 1 << distance) for i in range(lax.axis...  5.94 us
    unnamed x16, local copies, waits for them, and re-layouts  5.49 us
    gather x4, local copies, waits for them, and re-layouts, body(): chosen = jnp.take(partner, within, axis=0)  4.76 us
    dot_general x2, matrix products, hermitian_rows(): jnp.einsum('kpac,kpbc->kab', left_rows, half_done, preferred_element_type...  3.91 us
    reduce_scatter x1, local copies, waits for them, and re-layouts, body(): running = lax.psum_scatter(running, 'aux', scatter_dimension=2, tiled=True)  3.08 us
  transfers between devices with their start and end apart: 5, of which 3 were waited for; matrix products, arithmetic and copies ran while one was open for 12% of the time, Pallas kernels for 0%

commit v1 on v0

--- a/solution.py
+++ b/solution.py
@@ -1,13 +1,156 @@
+import functools
+
 import jax
 import jax.numpy as jnp
 from jax import lax
+from jax.experimental import pallas as pl
+from jax.experimental.pallas import tpu as pltpu
 from jax.sharding import PartitionSpec as P
 
+
 ROUNDS = 2
+VMEM_LIMIT = 24 << 20
 
 
 def from_partner(shard, axis, distance):
     return lax.ppermute(shard, axis, [(i, i ^ 1 << distance) for i in range(lax.axis_size(axis))])
+
+
+def from_sibling(shard):
+    return lax.ppermute(shard, "aux", [(0, 1), (1, 0)])
+
+
+def hop_round(index, blocks, wave):
+    top = index // (blocks // 4)
+    return (top + top // 2 + wave + 1) % 2
+
+
+def wave_targets(blocks, wave):
+    bit_count = blocks.bit_length() - 1
+    pairs = []
+    for index in range(blocks):
+        for which_round in range(ROUNDS):
+            partner = index ^ 1 << (bit_count - 1 - which_round)
+            if hop_round(partner, blocks, wave) == which_round:
+                pairs.append((index, partner))
+    return pairs
+
+
+def term_kernel(users, own_ref, sib_ref, mine_ref, other_ref, *rest, factor, wave, start, blocks):
+    if wave or start:
+        _, *rest = rest
+    out_ref, pair_buf, block_ref, half_ref, left_ref, total_ref, pair_sems, prev_sem, out_sem = rest
+    rows, width = mine_ref.shape[1:]
+    funcs, nao = own_ref.shape[2:4]
+    occupied = width // 2
+    core = lax.axis_index("aux")
+    which_round = hop_round(lax.axis_index("kpt"), blocks, wave)
+    spot = users[which_round, start]
+    loads = []
+    for which, pair_ref in enumerate((own_ref, sib_ref)):
+        for p in range(funcs):
+            q = which * funcs + p
+            loads.append(
+                pltpu.make_async_copy(
+                    pair_ref.at[which_round, spot, p], pair_buf.at[q], pair_sems.at[q]
+                )
+            )
+    for load in loads:
+        load.start()
+    if wave:
+        back = pltpu.make_async_copy(out_ref.at[spot], total_ref, prev_sem)
+        back.start()
+    for share, at in ((mine_ref, core), (other_ref, 1 - core)):
+        value = share[0]
+        top = pl.multiple_of(at * rows, rows)
+        block_ref[pl.ds(top, rows), :] = value
+        low = pl.multiple_of(nao + at * rows, rows)
+        block_ref[pl.ds(low, rows), :occupied] = -value[:, occupied:]
+        block_ref[pl.ds(low, rows), occupied:] = value[:, :occupied]
+    mine_at = pl.multiple_of(core * rows, rows)
+    for q in range(2 * funcs):
+        loads[q].wait()
+        half = jnp.dot(pair_buf[q], block_ref[...], preferred_element_type=jnp.float32)
+        half_ref[q] = half.astype(jnp.bfloat16)
+        left = half_ref[q, pl.ds(mine_at, rows), :]
+        left_ref[q, :rows, :] = left
+        left_ref[q, rows:, :occupied] = left[:, occupied:]
+        left_ref[q, rows:, occupied:] = -left[:, :occupied]
+    total = None
+    for q in range(2 * funcs):
+        part = lax.dot_general(
+            left_ref[q], half_ref[q], (((1,), (1,)), ((), ())), preferred_element_type=jnp.float32
+        )
+        total = part if total is None else total + part
+    total = (total * factor).reshape(2, rows, nao)
+    if wave:
+        back.wait()
+        total = total_ref[...] + total
+    total_ref[...] = total
+    store = pltpu.make_async_copy(total_ref, out_ref.at[spot], out_sem)
+    store.start()
+    store.wait()
+
+
+def add_terms(users, own, sib, mine, other, prev, factor, wave, start, blocks):
+    rows, width = mine.shape[1:]
+    per_device, funcs, nao = own.shape[1:4]
+    vmem = pl.BlockSpec(memory_space=pltpu.VMEM)
+    hbm = pl.BlockSpec(memory_space=pltpu.HBM)
+    operands = [users, own, sib, mine, other]
+    in_specs = [pl.BlockSpec(memory_space=pltpu.SMEM), hbm, hbm, vmem, vmem]
+    aliases = {}
+    if prev is not None:
+        aliases = {len(operands): 0}
+        operands.append(prev)
+        in_specs.append(hbm)
+    flops = funcs * 2 * (2 * nao * 2 * nao * width + 2 * 2 * rows * nao * width)
+    kernel = functools.partial(term_kernel, factor=factor, wave=wave, start=start, blocks=blocks)
+    return pl.pallas_call(
+        kernel,
+        out_shape=jax.ShapeDtypeStruct((per_device, 2, rows, nao), jnp.float32),
+        in_specs=in_specs,
+        out_specs=hbm,
+        scratch_shapes=[
+            pltpu.VMEM((2 * funcs, nao, 2 * nao), jnp.bfloat16),
+            pltpu.VMEM((2 * nao, width), jnp.bfloat16),
+            pltpu.VMEM((2 * funcs, nao, width), jnp.bfloat16),
+            pltpu.VMEM((2 * funcs, 2 * rows, width), jnp.bfloat16),
+            pltpu.VMEM((2, rows, nao), jnp.float32),
+            pltpu.SemaphoreType.DMA((2 * funcs,)),
+            pltpu.SemaphoreType.DMA,
+            pltpu.SemaphoreType.DMA,
+        ],
+        input_output_aliases=aliases,
+        compiler_params=pltpu.CompilerParams(vmem_limit_bytes=VMEM_LIMIT),
+        cost_estimate=pl.CostEstimate(flops=flops, transcendentals=0, bytes_accessed=6 << 20),
+    )(*operands)
+
+
+def paired_body(pair_tensors, orbitals, matchings):
+    per_device, nao, width = orbitals.shape
+    rows = nao // lax.axis_size("aux")
+    blocks = lax.axis_size("kpt")
+    factor = 1.0 / (ROUNDS * pair_tensors.shape[2] * lax.axis_size("aux") * (width // 2)) ** 0.5
+    offset = lax.axis_index("kpt") * per_device
+    piece = lax.dynamic_slice_in_dim(orbitals, lax.axis_index("aux") * rows, rows, 1)
+    within = lax.dynamic_slice_in_dim(matchings, offset, per_device, 1) % per_device
+    spots = jnp.arange(per_device, dtype=jnp.int32)
+    hits = within[:, None, :] == spots[None, :, None]
+    users = jnp.sum(jnp.where(hits, spots[None, None, :], 0), axis=2, dtype=jnp.int32)
+    arrived = []
+    sibling = from_sibling(pair_tensors)
+    for wave in range(ROUNDS):
+        targets = wave_targets(blocks, wave)
+        for start in range(per_device):
+            arrived.append((wave, start, lax.ppermute(piece[start : start + 1], "kpt", targets)))
+    running = None
+    for wave, start, mine in arrived:
+        other = from_sibling(mine)
+        running = add_terms(
+            users, pair_tensors, sibling, mine, other, running, factor, wave, start, blocks
+        )
+    return running
 
 
 def build_block(chosen):
@@ -35,29 +178,29 @@
     return jnp.stack([exch_real, exch_imag], axis=1)
 
 
-def body(pair_tensors, orbitals, matchings):
+def wide_body(pair_tensors, orbitals, matchings):
     per_device = orbitals.shape[0]
     occupied = orbitals.shape[2] // 2
     bit_count = lax.axis_size("kpt").bit_length() - 1
     factor = 1.0 / (ROUNDS * pair_tensors.shape[2] * lax.axis_size("aux") * occupied) ** 0.5
     offset = lax.axis_index("kpt") * per_device
+    stride = orbitals.shape[2] // lax.axis_size("aux")
+    piece = lax.dynamic_slice_in_dim(orbitals, lax.axis_index("aux") * stride, stride, 2)
     collected = []
     for which_round in range(ROUNDS):
-        swap_bit = bit_count - 1 - which_round
-        stride = orbitals.shape[2] // lax.axis_size("aux")
-        piece = lax.dynamic_slice_in_dim(orbitals, lax.axis_index("aux") * stride, stride, 2)
-        arrived = from_partner(piece, "kpt", swap_bit)
+        arrived = from_partner(piece, "kpt", bit_count - 1 - which_round)
         partner = lax.all_gather(arrived, "aux", axis=2, tiled=True)
         within = lax.dynamic_slice_in_dim(matchings[which_round], offset, per_device) % per_device
         chosen = jnp.take(partner, within, axis=0)
         half_done = half_transform(pair_tensors[which_round], build_block(chosen))
-        pieces = hermitian_rows(half_done, half_done) * factor
-        collected.append(pieces)
-    running = collected[0]
-    for extra in collected[1:]:
-        running = running + extra
-    running = lax.psum_scatter(running, "aux", scatter_dimension=2, tiled=True)
-    return running
+        collected.append(hermitian_rows(half_done, half_done) * factor)
+    return lax.psum_scatter(sum(collected), "aux", scatter_dimension=2, tiled=True)
+
+
+def body(pair_tensors, orbitals, matchings):
+    if lax.axis_size("aux") == 2 and lax.axis_size("kpt") % 4 == 0:
+        return paired_body(pair_tensors, orbitals, matchings)
+    return wide_body(pair_tensors, orbitals, matchings)
 
 
 def solution(mesh):

time: 102 us -> 57.6 us (0.56)
  waiting for transfers between devices: 46.7 us -> 21.9 us
  Pallas kernels: 0 us -> 23.5 us
  matrix products: 15.7 us -> 0 us
  between operations: 13.3 us -> 0.06 us
  local copies, waits for them, and re-layouts: 14.1 us -> 4.44 us
  other arithmetic: 5.37 us -> 0.9 us
    pallas_call x0 -> x4, Pallas kernels: none -> 23.5 us  [add_terms(): pl.pallas_call(kernel, out_shape=jax.ShapeDtypeStruct((per_device, 2, row...]
    dot_general x6 -> x0, matrix products: 15.7 us -> none  [the longest x2 9.16 us: half_transform(): jnp.einsum('kpab,kbc->kpac', pairs, block, preferred_element_type=jnp.flo...]
    reduce_scatter x1 -> x0, waiting for transfers between devices: 13.2 us -> none  [body(): running = lax.psum_scatter(running, 'aux', scatter_dimension=2, tiled=True)]
    ppermute x2 -> x9, waiting for transfers between devices: 33.4 us -> 21.9 us  [the longest x4 21.9 us: paired_body(): lax.ppermute(piece[start:start + 1], 'kpt', targets)]
    gather x4 -> x0, local copies, waits for them, and re-layouts: 4.76 us -> none  [body(): chosen = jnp.take(partner, within, axis=0)]
    reduce_scatter x1 -> x0, local copies, waits for them, and re-layouts: 3.08 us -> none  [body(): running = lax.psum_scatter(running, 'aux', scatter_dimension=2, tiled=True)]
    add x1 -> x0, other arithmetic: 2.97 us -> none  [body(): running = running + extra]
    unnamed x16 -> x2, local copies, waits for them, and re-layouts: 5.49 us -> 3.38 us
  transfers between devices with their start and end apart: 5 -> 9, of which waited for: 3 -> 4; matrix products, arithmetic and copies ran while one was open for 12% -> 3% of each run, Pallas kernels for 0% -> 31%
where the time goes in v1:
time: 57.6 us; the launch traced here: 57.1 us
  Pallas kernels  23.5 us (41%)
  waiting for transfers between devices  21.9 us (38%)
  starting transfers between devices  6.2 us (11%)
  local copies, waits for them, and re-layouts  4.44 us (8%)
  other arithmetic  0.9 us (2%)
    pallas_call x4, Pallas kernels, add_terms(): pl.pallas_call(kernel, out_shape=jax.ShapeDtypeStruct((per_device, 2, row...  23.5 us
    ppermute x4, waiting for transfers between devices, paired_body(): lax.ppermute(piece[start:start + 1], 'kpt', targets)  21.9 us
    ppermute x4, starting transfers between devices, paired_body(): lax.ppermute(piece[start:start + 1], 'kpt', targets)  5.68 us
    unnamed x2, local copies, waits for them, and re-layouts  3.38 us
  transfers between devices with their start and end apart: 9, of which 4 were waited for; matrix products, arithmetic and copies ran while one was open for 3% of the time, Pallas kernels for 31%

profile of v1, /device:TPU:0, one launch (start us, length us, event | category | flops | bytes accessed | tf_op | source)
XLA Modules:
  0.0 57.1 jit_solution(7691107131269352612)
XLA Ops:
  0.0 0.5 collective-permute-start
  0.5 1.1 %constant_dynamic-slice_fusion = (bf16[1,256,512]{2,1,0:T(8,128)(2,1)S(1)}, bf16[1,256,512]{2,1,0:T(8,128)(2,1)S(1)}) fusion(bf16[2,512,512]{2,1,0:T(8,128)(2,1)} %param.4, s32[]{:T(128)S(6)} %select_n.20, s32[]{:T(128)S(6)} %add.15), kind=kLoop, calls=%fused_computation.6 | loop fusion | bytes 1048584 | tf_op jit(solution)/shard_map/slice | solution.py:146
  1.6 3.6 %collective-permute-start.7 = (bf16[1,256,512]{2,1,0:T(8,128)(2,1)S(1)}, bf16[1,256,512]{2,1,0:T(8,128)(2,1)S(1)}, u32[]{:S(2)}, u32[]{:S(2)}) collective-permute-start(bf16[1,256,512]{2,1,0:T(8,128)(2,1)S(1)} %get-tuple-element.5), channel_id=1, source_target_pairs={{0,16},{2,18},{4,20},{6,22},{8,0},{10,2},{12,4},{14,6},{16,24},{18... | collective-permute-start | bytes 786440 | tf_op jit(solution)/shard_map/ppermute | solution.py:146
  5.2 1.6 %collective-permute-start.5 = (bf16[1,256,512]{2,1,0:T(8,128)(2,1)S(1)}, bf16[1,256,512]{2,1,0:T(8,128)(2,1)S(1)}, u32[]{:S(2)}, u32[]{:S(2)}) collective-permute-start(bf16[1,256,512]{2,1,0:T(8,128)(2,1)S(1)} %get-tuple-element.6), channel_id=1, source_target_pairs={{0,16},{2,18},{4,20},{6,22},{8,0},{10,2},{12,4},{14,6},{16,24},{18... | collective-permute-start | bytes 786440 | tf_op jit(solution)/shard_map/ppermute | solution.py:146
  6.8 0.4 collective-permute-start.3
  7.2 0.0 collective-permute-start.1
  7.2 4.7 %collective-permute-done.7.mine_ref = bf16[1,256,512]{2,1,0:T(8,128)(2,1)S(1)} collective-permute-done((bf16[1,256,512]{2,1,0:T(8,128)(2,1)S(1)}, bf16[1,256,512]{2,1,0:T(8,128)(2,1)S(1)}, u32[]{:S(2)}, u32[]{:S(2)}) %collective-permute-start.7) | collective-permute-done | bytes 262176 | tf_op jit(solution)/shard_map/ppermute | solution.py:146
  11.9 0.0 collective-permute-start.8
  11.9 0.8 %and_select_fusion = s32[2,2]{1,0:T(2,128)S(1)} fusion(s32[2,32]{1,0:T(2,128)} %param.5, s32[]{:T(128)S(6)} %select_n.17), kind=kLoop, calls=%fused_computation.4 | loop fusion | flops 44 | bytes 36 | tf_op jit(solution)/shard_map/jit(remainder)/select_n | solution.py:137
  12.7 0.1 fusion.users
  12.8 4.7 %collective-permute-done.5.mine_ref = bf16[1,256,512]{2,1,0:T(8,128)(2,1)S(1)} collective-permute-done((bf16[1,256,512]{2,1,0:T(8,128)(2,1)S(1)}, bf16[1,256,512]{2,1,0:T(8,128)(2,1)S(1)}, u32[]{:S(2)}, u32[]{:S(2)}) %collective-permute-start.5) | collective-permute-done | bytes 262176 | tf_op jit(solution)/shard_map/ppermute | solution.py:146
  17.5 0.0 collective-permute-start.6
  17.6 7.0 %collective-permute-done.3.mine_ref = bf16[1,256,512]{2,1,0:T(8,128)(2,1)S(1)} collective-permute-done((bf16[1,256,512]{2,1,0:T(8,128)(2,1)S(1)}, bf16[1,256,512]{2,1,0:T(8,128)(2,1)S(1)}, u32[]{:S(2)}, u32[]{:S(2)}) %collective-permute-start.3) | collective-permute-done | bytes 262176 | tf_op jit(solution)/shard_map/ppermute | solution.py:146
  24.6 5.5 %collective-permute-done.1.mine_ref = bf16[1,256,512]{2,1,0:T(8,128)(2,1)S(1)} collective-permute-done((bf16[1,256,512]{2,1,0:T(8,128)(2,1)S(1)}, bf16[1,256,512]{2,1,0:T(8,128)(2,1)S(1)}, u32[]{:S(2)}, u32[]{:S(2)}) %collective-permute-start.1) | collective-permute-done | bytes 262176 | tf_op jit(solution)/shard_map/ppermute | solution.py:146
  30.1 0.0 collective-permute-start.2
  30.1 0.0 collective-permute-done.sib_ref
  30.1 3.4 %copy-done = bf16[2,2,2,512,1024]{4,3,2,1,0:T(8,128)(2,1)S(1)} copy-done((bf16[2,2,2,512,1024]{4,3,2,1,0:T(8,128)(2,1)S(1)}, bf16[2,2,2,512,1024]{4,3,2,1,0:T(8,128)(2,1)}, u32[]{:S(2)}) %copy-start) | copy-done | bytes 8388632
  33.5 5.8 %shard_map.37.rest_0_ = f32[2,2,256,512]{3,2,1,0:T(8,128)} custom-call(s32[2,2]{1,0:T(2,128)S(1)} %fusion.users, bf16[2,2,2,512,1024]{4,3,2,1,0:T(8,128)(2,1)S(1)} %copy-done, bf16[2,2,2,512,1024]{4,3,2,1,0:T(8,128)(2,1)} %collective-permute-done.sib_ref, bf16[1,256,512]{2,1,0:T(8,128)(2,1)S(1)} %collective-permute-done.7.mine_ref, ...), custom_call_target="tpu_custom_call" | custom-call | flops 3221225472 | bytes 6291456 | tf_op jit(solution)/shard_map/pallas_call | solution.py:109
  39.3 0.0 collective-permute-done.6.other_ref
  39.3 5.8 %shard_map.38.rest_0_ = f32[2,2,256,512]{3,2,1,0:T(8,128)} custom-call(s32[2,2]{1,0:T(2,128)S(1)} %fusion.users, bf16[2,2,2,512,1024]{4,3,2,1,0:T(8,128)(2,1)S(1)} %copy-done, bf16[2,2,2,512,1024]{4,3,2,1,0:T(8,128)(2,1)} %collective-permute-done.sib_ref, bf16[1,256,512]{2,1,0:T(8,128)(2,1)S(1)} %collective-permute-done.5.mine_ref, ...), custom_call_target="tpu_custom_call", output_to_operand_aliasing={{}: (5, {})} | custom-call | flops 3221225472 | bytes 6291456 | tf_op jit(solution)/shard_map/pallas_call | solution.py:109
  45.1 0.0 collective-permute-done.4.other_ref
  45.2 5.9 %shard_map.39.rest_0_ = f32[2,2,256,512]{3,2,1,0:T(8,128)} custom-call(s32[2,2]{1,0:T(2,128)S(1)} %fusion.users, bf16[2,2,2,512,1024]{4,3,2,1,0:T(8,128)(2,1)S(1)} %copy-done, bf16[2,2,2,512,1024]{4,3,2,1,0:T(8,128)(2,1)} %collective-permute-done.sib_ref, bf16[1,256,512]{2,1,0:T(8,128)(2,1)S(1)} %collective-permute-done.3.mine_ref, ...), custom_call_target="tpu_custom_call", output_to_operand_aliasing={{}: (5, {})} | custom-call | flops 3221225472 | bytes 6291456 | tf_op jit(solution)/shard_map/pallas_call | solution.py:109
  51.1 0.0 collective-permute-done.2.other_ref
  51.1 5.9 %shard_map.40 = f32[2,2,256,512]{3,2,1,0:T(8,128)} custom-call(s32[2,2]{1,0:T(2,128)S(1)} %fusion.users, bf16[2,2,2,512,1024]{4,3,2,1,0:T(8,128)(2,1)S(1)} %copy-done, bf16[2,2,2,512,1024]{4,3,2,1,0:T(8,128)(2,1)} %collective-permute-done.sib_ref, bf16[1,256,512]{2,1,0:T(8,128)(2,1)S(1)} %collective-permute-done.1.mine_ref, ...), custom_call_target="tpu_custom_call", output_to_operand_aliasing={{}: (5, {})} | custom-call | flops 3221225472 | bytes 6291456 | tf_op jit(solution)/shard_map/pallas_call | solution.py:109
  (3 shorter events, 0.0 us)
Async XLA Ops:
  0.0 30.1 %collective-permute-start = (bf16[2,2,2,512,1024]{4,3,2,1,0:T(8,128)(2,1)}, bf16[2,2,2,512,1024]{4,3,2,1,0:T(8,128)(2,1)}, u32[]{:S(2)}, u32[]{:S(2)}) collective-permute-start(bf16[2,2,2,512,1024]{4,3,2,1,0:T(8,128)(2,1)} %own_ref.7), channel_id=1, source_target_pairs={{0,1},{1,0},{2,3},{3,2},{4,5},{5,4},{6,7},{7,6},{8,9},{9,8},{10,11... | collective-permute-start | bytes 25165832 | tf_op jit(solution)/shard_map/ppermute | solution.py:20
  1.6 10.4 %collective-permute-start.7 = (bf16[1,256,512]{2,1,0:T(8,128)(2,1)S(1)}, bf16[1,256,512]{2,1,0:T(8,128)(2,1)S(1)}, u32[]{:S(2)}, u32[]{:S(2)}) collective-permute-start(bf16[1,256,512]{2,1,0:T(8,128)(2,1)S(1)} %get-tuple-element.5), channel_id=1, source_target_pairs={{0,16},{2,18},{4,20},{6,22},{8,0},{10,2},{12,4},{14,6},{16,24},{18... | collective-permute-start | bytes 786440 | tf_op jit(solution)/shard_map/ppermute | solution.py:146
  5.2 12.4 %collective-permute-start.5 = (bf16[1,256,512]{2,1,0:T(8,128)(2,1)S(1)}, bf16[1,256,512]{2,1,0:T(8,128)(2,1)S(1)}, u32[]{:S(2)}, u32[]{:S(2)}) collective-permute-start(bf16[1,256,512]{2,1,0:T(8,128)(2,1)S(1)} %get-tuple-element.6), channel_id=1, source_target_pairs={{0,16},{2,18},{4,20},{6,22},{8,0},{10,2},{12,4},{14,6},{16,24},{18... | collective-permute-start | bytes 786440 | tf_op jit(solution)/shard_map/ppermute | solution.py:146
  6.8 17.8 %collective-permute-start.3 = (bf16[1,256,512]{2,1,0:T(8,128)(2,1)S(1)}, bf16[1,256,512]{2,1,0:T(8,128)(2,1)S(1)}, u32[]{:S(2)}, u32[]{:S(2)}) collective-permute-start(bf16[1,256,512]{2,1,0:T(8,128)(2,1)S(1)} %get-tuple-element.5), channel_id=1, source_target_pairs={{0,8},{2,10},{4,12},{6,14},{8,24},{10,26},{12,28},{14,30},{16,0},{... | collective-permute-start | bytes 786440 | tf_op jit(solution)/shard_map/ppermute | solution.py:146
  7.2 22.9 %collective-permute-start.1 = (bf16[1,256,512]{2,1,0:T(8,128)(2,1)S(1)}, bf16[1,256,512]{2,1,0:T(8,128)(2,1)S(1)}, u32[]{:S(2)}, u32[]{:S(2)}) collective-permute-start(bf16[1,256,512]{2,1,0:T(8,128)(2,1)S(1)} %get-tuple-element.6), channel_id=1, source_target_pairs={{0,8},{2,10},{4,12},{6,14},{8,24},{10,26},{12,28},{14,30},{16,0},{... | collective-permute-start | bytes 786440 | tf_op jit(solution)/shard_map/ppermute | solution.py:146
  11.9 18.2 %collective-permute-start.8 = (bf16[1,256,512]{2,1,0:T(8,128)(2,1)S(1)}, bf16[1,256,512]{2,1,0:T(8,128)(2,1)S(1)}, u32[]{:S(2)}, u32[]{:S(2)}) collective-permute-start(bf16[1,256,512]{2,1,0:T(8,128)(2,1)S(1)} %collective-permute-done.7.mine_ref), channel_id=1, source_target_pairs={{0,1},{1,0},{2,3},{3,2},{4,5},{5,4},{6,7},{7,6},{8,9},{9,8},{10,11... | collective-permute-start | bytes 786440 | tf_op jit(solution)/shard_map/ppermute | solution.py:20
  17.5 21.8 %collective-permute-start.6 = (bf16[1,256,512]{2,1,0:T(8,128)(2,1)S(1)}, bf16[1,256,512]{2,1,0:T(8,128)(2,1)S(1)}, u32[]{:S(2)}, u32[]{:S(2)}) collective-permute-start(bf16[1,256,512]{2,1,0:T(8,128)(2,1)S(1)} %collective-permute-done.5.mine_ref), channel_id=1, source_target_pairs={{0,1},{1,0},{2,3},{3,2},{4,5},{5,4},{6,7},{7,6},{8,9},{9,8},{10,11... | collective-permute-start | bytes 786440 | tf_op jit(solution)/shard_map/ppermute | solution.py:20
  24.6 20.6 %collective-permute-start.4 = (bf16[1,256,512]{2,1,0:T(8,128)(2,1)S(1)}, bf16[1,256,512]{2,1,0:T(8,128)(2,1)S(1)}, u32[]{:S(2)}, u32[]{:S(2)}) collective-permute-start(bf16[1,256,512]{2,1,0:T(8,128)(2,1)S(1)} %collective-permute-done.3.mine_ref), channel_id=1, source_target_pairs={{0,1},{1,0},{2,3},{3,2},{4,5},{5,4},{6,7},{7,6},{8,9},{9,8},{10,11... | collective-permute-start | bytes 786440 | tf_op jit(solution)/shard_map/ppermute | solution.py:20
  30.1 21.0 %collective-permute-start.2 = (bf16[1,256,512]{2,1,0:T(8,128)(2,1)S(1)}, bf16[1,256,512]{2,1,0:T(8,128)(2,1)S(1)}, u32[]{:S(2)}, u32[]{:S(2)}) collective-permute-start(bf16[1,256,512]{2,1,0:T(8,128)(2,1)S(1)} %collective-permute-done.1.mine_ref), channel_id=1, source_target_pairs={{0,1},{1,0},{2,3},{3,2},{4,5},{5,4},{6,7},{7,6},{8,9},{9,8},{10,11... | collective-permute-start | bytes 786440 | tf_op jit(solution)/shard_map/ppermute | solution.py:20
  30.1 3.4 %copy-start = (bf16[2,2,2,512,1024]{4,3,2,1,0:T(8,128)(2,1)S(1)}, bf16[2,2,2,512,1024]{4,3,2,1,0:T(8,128)(2,1)}, u32[]{:S(2)}) copy-start(bf16[2,2,2,512,1024]{4,3,2,1,0:T(8,128)(2,1)} %own_ref.7) | copy-start | bytes 25165828

commit v2 on v0

--- a/solution.py
+++ b/solution.py
@@ -1,13 +1,246 @@
+import functools
+
 import jax
 import jax.numpy as jnp
 from jax import lax
+from jax.experimental import pallas as pl
+from jax.experimental.pallas import tpu as pltpu
 from jax.sharding import PartitionSpec as P
 
+
 ROUNDS = 2
+PARTS = 2
+VMEM_LIMIT = 12 << 20
+STAGE_LIMIT = 55 << 20
+SMEM = pl.BlockSpec(memory_space=pltpu.SMEM)
+VMEM = pl.BlockSpec(memory_space=pltpu.VMEM)
+HBM = pl.BlockSpec(memory_space=pltpu.HBM)
 
 
 def from_partner(shard, axis, distance):
     return lax.ppermute(shard, axis, [(i, i ^ 1 << distance) for i in range(lax.axis_size(axis))])
+
+
+def from_sibling(shard):
+    return lax.ppermute(shard, "aux", [(0, 1), (1, 0)])
+
+
+def hop_round(index, blocks, wave):
+    top = index // (blocks // 4)
+    return (top + top // 2 + wave + 1) % 2
+
+
+def wave_targets(blocks, wave):
+    bit_count = blocks.bit_length() - 1
+    pairs = []
+    for index in range(blocks):
+        for which_round in range(ROUNDS):
+            partner = index ^ 1 << (bit_count - 1 - which_round)
+            if hop_round(partner, blocks, wave) == which_round:
+                pairs.append((index, partner))
+    return pairs
+
+
+def stage_kernel(users, pair_ref, *rest, blocks):
+    out_refs, slot_ref, sems = rest[:ROUNDS], rest[ROUNDS], rest[-1]
+    core = lax.axis_index("aux")
+    index = lax.axis_index("kpt")
+    loads = []
+    for wave, out_ref in enumerate(out_refs):
+        source = pair_ref.at[hop_round(index, blocks, wave), users[wave, core]]
+        loads.append(pltpu.make_async_copy(source, out_ref, sems.at[wave]))
+        loads[-1].start()
+    for side, at in enumerate((core, 1 - core)):
+        slot_ref[side] = jnp.full(slot_ref.shape[1:], users[ROUNDS - 1, at], jnp.int32)
+    for load in loads:
+        load.wait()
+
+
+def stage(users, pair_tensors, blocks):
+    shape = jax.ShapeDtypeStruct(pair_tensors.shape[2:], pair_tensors.dtype)
+    slots = jax.ShapeDtypeStruct((2, 8, 128), jnp.int32)
+    return pl.pallas_call(
+        functools.partial(stage_kernel, blocks=blocks),
+        out_shape=(shape,) * ROUNDS + (slots,),
+        in_specs=[SMEM, HBM],
+        out_specs=(VMEM,) * (ROUNDS + 1),
+        scratch_shapes=[pltpu.SemaphoreType.DMA((ROUNDS,))],
+        compiler_params=pltpu.CompilerParams(vmem_limit_bytes=STAGE_LIMIT),
+        name="stage",
+    )(users, pair_tensors)
+
+
+def term_kernel(*rest, factor, wave, part, fetch, earlier, blocks):
+    users = None
+    if not (wave and part):
+        users, *rest = rest
+    own_ref, sib_ref, mine_ref, *rest = rest
+    sources, rest = rest[:earlier], rest[earlier:]
+    if fetch is not None:
+        full_ref, out_ref, got_ref, block_ref, left_ref, sem = (sib_ref, *rest)
+        if part:
+            full_ref, sources = sources[-1], sources[:-1]
+    elif wave and part:
+        out_ref, send_ref, block_ref, left_ref = rest
+    else:
+        out_ref, block_ref, left_ref = rest
+    nao, width = mine_ref.shape
+    funcs = own_ref.shape[0]
+    occupied = width // 2
+    core = lax.axis_index("aux")
+    if fetch is not None:
+        which_round = hop_round(lax.axis_index("kpt"), blocks, fetch)
+        load = pltpu.make_async_copy(full_ref.at[which_round, users[fetch, core]], got_ref, sem)
+        load.start()
+    block_ref[:nao, :] = mine_ref[...]
+    block_ref[nao:, :occupied] = -mine_ref[:, occupied:]
+    block_ref[nao:, occupied:] = mine_ref[:, :occupied]
+    for q in range(2 * funcs):
+        if q < funcs:
+            pair = own_ref[q]
+        elif fetch == wave:
+            if q == funcs:
+                load.wait()
+            pair = got_ref[q - funcs]
+        else:
+            pair = sib_ref[q - funcs]
+        half = jnp.dot(pair, block_ref[...], preferred_element_type=jnp.float32)
+        half = half.astype(jnp.bfloat16)
+        at = q * width
+        left_ref[0, :, at : at + width] = half
+        left_ref[1, :, at : at + occupied] = half[:, occupied:]
+        left_ref[1, :, at + occupied : at + width] = -half[:, :occupied]
+    if len(sources) == 2:
+        same = users[wave - 1, core] == users[wave, core]
+    for kind in range(2):
+        total = lax.dot_general(
+            left_ref[kind], left_ref[0], (((1,), (1,)), ((), ())), preferred_element_type=jnp.float32
+        )
+        total = total * factor
+        if len(sources) == 1:
+            total = sources[0][kind] + total
+        if len(sources) == 2:
+            total = jnp.where(same, sources[0][kind], sources[1][kind]) + total
+        if wave and part:
+            rows = out_ref.shape[1]
+            flip = core == 0
+            out_ref[kind] = jnp.where(flip, total[:rows], total[rows:])
+            send_ref[kind] = jnp.where(flip, total[rows:], total[:rows])
+        else:
+            out_ref[kind] = total
+    if fetch is not None and fetch != wave:
+        load.wait()
+
+
+def add_terms(users, own, sib, mine, sources, full, factor, wave, part, blocks):
+    nao, width = mine.shape
+    funcs = own.shape[0]
+    whole = jax.ShapeDtypeStruct((2, nao, nao), jnp.float32)
+    rows_shape = jax.ShapeDtypeStruct((2, nao // 2, nao), jnp.float32)
+    pair_shape = jax.ShapeDtypeStruct(own.shape, own.dtype)
+    fetch = {(0, 0): 0, (0, 1): 1}.get((wave, part))
+    scratch = [
+        pltpu.VMEM((2 * nao, width), jnp.bfloat16),
+        pltpu.VMEM((2, nao, 2 * funcs * width), jnp.bfloat16),
+    ]
+    if fetch is None:
+        out_shape = (rows_shape, rows_shape) if part else (whole,)
+    else:
+        out_shape = (whole, pair_shape)
+        scratch.append(pltpu.SemaphoreType.DMA)
+    operands = [users, own, full if fetch == 0 else sib, mine, *sources]
+    in_specs = [SMEM, VMEM, HBM if fetch == 0 else VMEM, VMEM] + [VMEM] * len(sources)
+    if fetch == 1:
+        operands.append(full)
+        in_specs.append(HBM)
+    flops = funcs * 2 * (2 * nao * 2 * nao * width + 2 * 2 * nao * nao * width)
+    kernel = functools.partial(
+        term_kernel,
+        factor=factor,
+        wave=wave,
+        part=part,
+        fetch=fetch,
+        earlier=len(operands) - 4,
+        blocks=blocks,
+    )
+    if fetch is None and part:
+        operands, in_specs = operands[1:], in_specs[1:]
+    return pl.pallas_call(
+        kernel,
+        out_shape=out_shape,
+        in_specs=in_specs,
+        out_specs=(VMEM,) * len(out_shape),
+        scratch_shapes=scratch,
+        compiler_params=pltpu.CompilerParams(vmem_limit_bytes=VMEM_LIMIT),
+        cost_estimate=pl.CostEstimate(flops=flops, transcendentals=0, bytes_accessed=6 << 20),
+    )(*operands)
+
+
+def place_kernel(slot_ref, got_ref, *rest, side):
+    out_ref, sem = rest[-2:]
+    spot = jnp.max(slot_ref[side])
+    store = pltpu.make_async_copy(got_ref, out_ref.at[spot], sem)
+    store.start()
+    store.wait()
+
+
+def place(slots, got, partial_out, per_device):
+    operands = [slots, got]
+    in_specs = [VMEM, VMEM]
+    aliases = {}
+    if partial_out is not None:
+        operands.append(partial_out)
+        in_specs.append(HBM)
+        aliases = {2: 0}
+    return pl.pallas_call(
+        functools.partial(place_kernel, side=len(aliases)),
+        out_shape=jax.ShapeDtypeStruct((per_device,) + got.shape, got.dtype),
+        in_specs=in_specs,
+        out_specs=HBM,
+        scratch_shapes=[pltpu.SemaphoreType.DMA],
+        input_output_aliases=aliases,
+        compiler_params=pltpu.CompilerParams(vmem_limit_bytes=VMEM_LIMIT),
+        name="place",
+    )(*operands)
+
+
+def paired_body(pair_tensors, orbitals, matchings):
+    per_device, _, width = orbitals.shape
+    occupied = width // 2
+    blocks = lax.axis_size("kpt")
+    factor = 1.0 / (ROUNDS * pair_tensors.shape[2] * lax.axis_size("aux") * occupied) ** 0.5
+    offset = lax.axis_index("kpt") * per_device
+    share = occupied // PARTS
+    piece = lax.dynamic_index_in_dim(orbitals, lax.axis_index("aux"), 0, keepdims=False)
+    sib = from_sibling(pair_tensors)
+    arrived = []
+    for wave in range(ROUNDS):
+        targets = wave_targets(blocks, wave)
+        for part in range(PARTS):
+            real_part = piece[:, part * share : (part + 1) * share]
+            imag_part = piece[:, occupied + part * share : occupied + (part + 1) * share]
+            chunk = jnp.concatenate([real_part, imag_part], axis=1)
+            arrived.append((wave, part, lax.ppermute(chunk, "kpt", targets)))
+    within = lax.dynamic_slice_in_dim(matchings, offset, per_device, 1) % per_device
+    spots = jnp.arange(per_device, dtype=jnp.int32)
+    hits = within[:, None, :] == spots[None, :, None]
+    users = jnp.sum(jnp.where(hits, spots[None, None, :], 0), axis=2, dtype=jnp.int32)
+    first_round = hop_round(lax.axis_index("kpt"), blocks, 0)
+    users = jnp.where(first_round == 0, users, users[::-1])
+    *own, slots = stage(users, pair_tensors, blocks)
+    sources = []
+    near = None
+    for wave, part, mine in arrived:
+        got = add_terms(users, own[wave], near, mine, sources, sib, factor, wave, part, blocks)
+        if wave == 0 and part == 0:
+            near = got[1]
+        sources = [got[0]]
+        if wave == 0 and part == PARTS - 1:
+            near = got[1]
+            sources = [got[0], from_sibling(got[0])]
+    received = from_sibling(got[1])
+    kept = place(slots, got[0], None, per_device)
+    return place(slots, received, kept, per_device)
 
 
 def build_block(chosen):
@@ -35,29 +268,30 @@
     return jnp.stack([exch_real, exch_imag], axis=1)
 
 
-def body(pair_tensors, orbitals, matchings):
+def wide_body(pair_tensors, orbitals, matchings):
     per_device = orbitals.shape[0]
     occupied = orbitals.shape[2] // 2
     bit_count = lax.axis_size("kpt").bit_length() - 1
     factor = 1.0 / (ROUNDS * pair_tensors.shape[2] * lax.axis_size("aux") * occupied) ** 0.5
     offset = lax.axis_index("kpt") * per_device
+    stride = orbitals.shape[2] // lax.axis_size("aux")
+    piece = lax.dynamic_slice_in_dim(orbitals, lax.axis_index("aux") * stride, stride, 2)
     collected = []
     for which_round in range(ROUNDS):
-        swap_bit = bit_count - 1 - which_round
-        stride = orbitals.shape[2] // lax.axis_size("aux")
-        piece = lax.dynamic_slice_in_dim(orbitals, lax.axis_index("aux") * stride, stride, 2)
-        arrived = from_partner(piece, "kpt", swap_bit)
+        arrived = from_partner(piece, "kpt", bit_count - 1 - which_round)
         partner = lax.all_gather(arrived, "aux", axis=2, tiled=True)
         within = lax.dynamic_slice_in_dim(matchings[which_round], offset, per_device) % per_device
         chosen = jnp.take(partner, within, axis=0)
         half_done = half_transform(pair_tensors[which_round], build_block(chosen))
-        pieces = hermitian_rows(half_done, half_done) * factor
-        collected.append(pieces)
-    running = collected[0]
-    for extra in collected[1:]:
-        running = running + extra
-    running = lax.psum_scatter(running, "aux", scatter_dimension=2, tiled=True)
-    return running
+        collected.append(hermitian_rows(half_done, half_done) * factor)
+    return lax.psum_scatter(sum(collected), "aux", scatter_dimension=2, tiled=True)
+
+
+def body(pair_tensors, orbitals, matchings):
+    shares = orbitals.shape[0]
+    if lax.axis_size("aux") == shares == 2 and lax.axis_size("kpt") % 4 == 0:
+        return paired_body(pair_tensors, orbitals, matchings)
+    return wide_body(pair_tensors, orbitals, matchings)
 
 
 def solution(mesh):

time: 102 us -> 46.5 us (0.46)
  waiting for transfers between devices: 46.7 us -> 9.79 us
  Pallas kernels: 0 us -> 20.8 us
  matrix products: 15.7 us -> 0 us
  between operations: 13.3 us -> 0.18 us
  local copies, waits for them, and re-layouts: 14.1 us -> 2.49 us
  starting transfers between devices: 6.02 us -> 12 us
  other arithmetic: 5.37 us -> 0.87 us
    ppermute x2 -> x7, waiting for transfers between devices: 33.4 us -> 9.79 us  [the longest x4 7.9 us: paired_body(): arrived.append((wave, part, lax.ppermute(chunk, 'kpt', targets)))]
    pallas_call x0 -> x7, Pallas kernels: none -> 20.8 us  [the longest x4 13.4 us: add_terms(): pl.pallas_call(kernel, out_shape=out_shape, in_specs=in_specs, out_specs=...]
    dot_general x6 -> x0, matrix products: 15.7 us -> none  [the longest x2 9.16 us: half_transform(): jnp.einsum('kpab,kbc->kpac', pairs, block, preferred_element_type=jnp.flo...]
    reduce_scatter x1 -> x0, waiting for transfers between devices: 13.2 us -> none  [body(): running = lax.psum_scatter(running, 'aux', scatter_dimension=2, tiled=True)]
    ppermute x2 -> x7, starting transfers between devices: 5.94 us -> 12 us  [the longest x4 11 us: paired_body(): arrived.append((wave, part, lax.ppermute(chunk, 'kpt', targets)))]
    gather x4 -> x0, local copies, waits for them, and re-layouts: 4.76 us -> none  [body(): chosen = jnp.take(partner, within, axis=0)]
    unnamed x16 -> x12, local copies, waits for them, and re-layouts: 5.49 us -> 2.34 us
    reduce_scatter x1 -> x0, local copies, waits for them, and re-layouts: 3.08 us -> none  [body(): running = lax.psum_scatter(running, 'aux', scatter_dimension=2, tiled=True)]
  transfers between devices with their start and end apart: 5 -> 7, of which waited for: 3 -> 4; matrix products, arithmetic and copies ran while one was open for 12% -> 2% of each run, Pallas kernels for 0% -> 30%
where the time goes in v2:
time: 46.5 us; the launch traced here: 46.2 us
  Pallas kernels  20.8 us (45%)
  starting transfers between devices  12 us (26%)
  waiting for transfers between devices  9.79 us (21%)
  local copies, waits for them, and re-layouts  2.49 us (5%)
  other arithmetic  0.87 us (2%)
    pallas_call x4, Pallas kernels, add_terms(): pl.pallas_call(kernel, out_shape=out_shape, in_specs=in_specs, out_specs=...  13.4 us
    ppermute x4, starting transfers between devices, paired_body(): arrived.append((wave, part, lax.ppermute(chunk, 'kpt', targets)))  11 us
    ppermute x4, waiting for transfers between devices, paired_body(): arrived.append((wave, part, lax.ppermute(chunk, 'kpt', targets)))  7.9 us
    pallas_call x1, Pallas kernels, stage(): pl.pallas_call(functools.partial(stage_kernel, blocks=blocks), out_shape=...  5.1 us
    pallas_call x2, Pallas kernels, place(): pl.pallas_call(functools.partial(place_kernel, side=len(aliases)), out_sh...  2.35 us
    unnamed x12, local copies, waits for them, and re-layouts  2.34 us
    ppermute x3, waiting for transfers between devices, from_sibling(): return lax.ppermute(shard, 'aux', [(0, 1), (1, 0)])  1.89 us
    ppermute x3, starting transfers between devices, from_sibling(): return lax.ppermute(shard, 'aux', [(0, 1), (1, 0)])  1 us
  transfers between devices with their start and end apart: 7, of which 4 were waited for; matrix products, arithmetic and copies ran while one was open for 2% of the time, Pallas kernels for 30%

profile of v2, /device:TPU:0, one launch (start us, length us, event | category | flops | bytes accessed | tf_op | source)
XLA Modules:
  0.0 46.2 jit_solution(7466189105958043216)
XLA Ops:
  0.0 0.5 %collective-permute-start = (bf16[2,2,2,512,1024]{4,3,2,1,0:T(8,128)(2,1)}, bf16[2,2,2,512,1024]{4,3,2,1,0:T(8,128)(2,1)}, u32[]{:S(2)}, u32[]{:S(2)}) collective-permute-start(bf16[2,2,2,512,1024]{4,3,2,1,0:T(8,128)(2,1)} %pair_ref.1), channel_id=1, source_target_pairs={{0,1},{1,0},{2,3},{3,2},{4,5},{5,4},{6,7},{7,6},{8,9},{9,8},{10,11... | collective-permute-start | bytes 25165832 | tf_op jit(solution)/shard_map/ppermute | solution.py:25
  0.5 0.7 %copy-done = bf16[2,512,512]{2,1,0:T(8,128)(2,1)S(1)} copy-done((bf16[2,512,512]{2,1,0:T(8,128)(2,1)S(1)}, bf16[2,512,512]{2,1,0:T(8,128)(2,1)}, u32[]{:S(2)}) %copy-start) | copy-done | bytes 1048600
  1.3 0.1 fusion.2
  1.4 4.1 %collective-permute-start.1 = (bf16[512,256]{1,0:T(8,128)(2,1)S(1)}, bf16[512,256]{1,0:T(8,128)(2,1)S(1)}, u32[]{:S(2)}, u32[]{:S(2)}) collective-permute-start(bf16[512,256]{1,0:T(8,128)(2,1)S(1)} %pad_maximum_fusion), channel_id=1, source_target_pairs={{0,16},{2,18},{4,20},{6,22},{8,0},{10,2},{12,4},{14,6},{16,24},{18... | collective-permute-start | bytes 786440 | tf_op jit(solution)/shard_map/ppermute | solution.py:223
  5.6 1.6 %collective-permute-start.2 = (bf16[512,256]{1,0:T(8,128)(2,1)S(1)}, bf16[512,256]{1,0:T(8,128)(2,1)S(1)}, u32[]{:S(2)}, u32[]{:S(2)}) collective-permute-start(bf16[512,256]{1,0:T(8,128)(2,1)S(1)} %pad_maximum_fusion.1), channel_id=1, source_target_pairs={{0,16},{2,18},{4,20},{6,22},{8,0},{10,2},{12,4},{14,6},{16,24},{18... | collective-permute-start | bytes 786440 | tf_op jit(solution)/shard_map/ppermute | solution.py:223
  7.2 0.1 and_select_fusion
  7.3 0.1 fusion
  7.5 0.6 %broadcast_select_fusion.users.rest_0_ = s32[2,2]{1,0:T(2,128)} fusion(s32[2,2]{1,0:T(2,128)S(1)} %fusion, s32[2,2]{1,0:T(2,128)S(1)} %rev.3, pred[]{:T(512)S(6)} %eq.20), kind=kLoop, calls=%fused_computation.9 | loop fusion | flops 4 | bytes 49 | tf_op jit(solution)/shard_map/jit(_where)/select_n | solution.py:229
  8.1 5.1 %stage.1 = (bf16[2,512,1024]{2,1,0:T(8,128)(2,1)}, bf16[2,512,1024]{2,1,0:T(8,128)(2,1)}, s32[2,8,128]{2,1,0:T(8,128)}) custom-call(s32[2,2]{1,0:T(2,128)} %broadcast_select_fusion.users.rest_0_, bf16[2,2,2,512,1024]{4,3,2,1,0:T(8,128)(2,1)} %pair_ref.1), custom_call_target="tpu_custom_call" | custom-call | tf_op jit(solution)/shard_map/stage/pallas_call | solution.py:62
  13.2 0.4 collective-permute-done.rest_2_.rest_5_
  13.6 1.6 %copy-done.1 = bf16[2,512,1024]{2,1,0:T(8,128)(2,1)S(1)} copy-done((bf16[2,512,1024]{2,1,0:T(8,128)(2,1)S(1)}, bf16[2,512,1024]{2,1,0:T(8,128)(2,1)}, u32[]{:S(2)}) %copy-start.1) | copy-done | bytes 2097176
  15.2 4.6 %shard_map.37 = (f32[2,512,512]{2,1,0:T(8,128)S(1)}, bf16[2,512,1024]{2,1,0:T(8,128)(2,1)S(1)}) custom-call(s32[2,2]{1,0:T(2,128)S(1)} %copy-done.4, bf16[2,512,1024]{2,1,0:T(8,128)(2,1)S(1)} %copy-done.1, bf16[2,2,2,512,1024]{4,3,2,1,0:T(8,128)(2,1)} %collective-permute-done.rest_2_.rest_5_, bf16[512,256]{1,0:T(8,128)(2,1)S(1)} %collective-permute-done.1.rest_3_), custom_call_target="tpu_custom_call" | custom-call | flops 2147483648 | bytes 6291456 | tf_op jit(solution)/shard_map/pallas_call | solution.py:168
  19.8 3.3 %shard_map.38 = (f32[2,512,512]{2,1,0:T(8,128)S(1)}, bf16[2,512,1024]{2,1,0:T(8,128)(2,1)S(1)}) custom-call(s32[2,2]{1,0:T(2,128)S(1)} %copy-done.4, bf16[2,512,1024]{2,1,0:T(8,128)(2,1)S(1)} %copy-done.1, bf16[2,512,1024]{2,1,0:T(8,128)(2,1)S(1)} %get-tuple-element.17.rest_2_, bf16[512,256]{1,0:T(8,128)(2,1)S(1)} %collective-permute-done.2.rest_3_, ...), custom_call_target="tpu_custom_call" | custom-call | flops 2147483648 | bytes 6291456 | tf_op jit(solution)/shard_map/pallas_call | solution.py:168
  23.2 0.4 collective-permute-start.5
  23.6 2.7 %collective-permute-start.4 = (bf16[512,256]{1,0:T(8,128)(2,1)S(1)}, bf16[512,256]{1,0:T(8,128)(2,1)S(1)}, u32[]{:S(2)}, u32[]{:S(2)}) collective-permute-start(bf16[512,256]{1,0:T(8,128)(2,1)S(1)} %pad_maximum_fusion), channel_id=1, source_target_pairs={{0,8},{2,10},{4,12},{6,14},{8,24},{10,26},{12,28},{14,30},{16,0},{... | collective-permute-start | bytes 786440 | tf_op jit(solution)/shard_map/ppermute | solution.py:223
  26.3 2.6 %collective-permute-start.3 = (bf16[512,256]{1,0:T(8,128)(2,1)S(1)}, bf16[512,256]{1,0:T(8,128)(2,1)S(1)}, u32[]{:S(2)}, u32[]{:S(2)}) collective-permute-start(bf16[512,256]{1,0:T(8,128)(2,1)S(1)} %pad_maximum_fusion.1), channel_id=1, source_target_pairs={{0,8},{2,10},{4,12},{6,14},{8,24},{10,26},{12,28},{14,30},{16,0},{... | collective-permute-start | bytes 786440 | tf_op jit(solution)/shard_map/ppermute | solution.py:223
  28.9 5.6 %collective-permute-done.4.rest_3_ = bf16[512,256]{1,0:T(8,128)(2,1)S(1)} collective-permute-done((bf16[512,256]{1,0:T(8,128)(2,1)S(1)}, bf16[512,256]{1,0:T(8,128)(2,1)S(1)}, u32[]{:S(2)}, u32[]{:S(2)}) %collective-permute-start.4) | collective-permute-done | bytes 262176 | tf_op jit(solution)/shard_map/ppermute | solution.py:223
  34.5 3.0 %shard_map.39.rest_3_ = f32[2,512,512]{2,1,0:T(8,128)S(1)} custom-call(s32[2,2]{1,0:T(2,128)S(1)} %copy-done.4, bf16[2,512,1024]{2,1,0:T(8,128)(2,1)S(1)} %copy-done.2, bf16[2,512,1024]{2,1,0:T(8,128)(2,1)S(1)} %get-tuple-element.19.rest_2_.rest_1_, bf16[512,256]{1,0:T(8,128)(2,1)S(1)} %collective-permute-done.4.rest_3_, ...), custom_call_target="tpu_custom_call" | custom-call | flops 2147483648 | bytes 6291456 | tf_op jit(solution)/shard_map/pallas_call | solution.py:168
  37.5 2.3 %collective-permute-done.3.rest_2_ = bf16[512,256]{1,0:T(8,128)(2,1)S(1)} collective-permute-done((bf16[512,256]{1,0:T(8,128)(2,1)S(1)}, bf16[512,256]{1,0:T(8,128)(2,1)S(1)}, u32[]{:S(2)}, u32[]{:S(2)}) %collective-permute-start.3) | collective-permute-done | bytes 262176 | tf_op jit(solution)/shard_map/ppermute | solution.py:223
  39.8 2.5 %shard_map.40 = (f32[2,256,512]{2,1,0:T(8,128)S(1)}, f32[2,256,512]{2,1,0:T(8,128)S(1)}) custom-call(bf16[2,512,1024]{2,1,0:T(8,128)(2,1)S(1)} %copy-done.2, bf16[2,512,1024]{2,1,0:T(8,128)(2,1)S(1)} %get-tuple-element.19.rest_2_.rest_1_, bf16[512,256]{1,0:T(8,128)(2,1)S(1)} %collective-permute-done.3.rest_2_, f32[2,512,512]{2,1,0:T(8,128)S(1)} %shard_map.39.rest_3_), custom_call_target="tpu_custom_call" | custom-call | flops 2147483648 | bytes 6291456 | tf_op jit(solution)/shard_map/pallas_call | solution.py:168
  42.3 0.1 collective-permute-start.6
  42.4 1.2 %place.2.rest_0_ = f32[2,2,256,512]{3,2,1,0:T(8,128)} custom-call(s32[2,8,128]{2,1,0:T(8,128)S(1)} %copy-done.3, f32[2,256,512]{2,1,0:T(8,128)S(1)} %get-tuple-element.22.got_ref), custom_call_target="tpu_custom_call" | custom-call | tf_op jit(solution)/shard_map/place/pallas_call | solution.py:195
  43.6 1.5 %collective-permute-done.6.got_ref = f32[2,256,512]{2,1,0:T(8,128)S(1)} collective-permute-done((f32[2,256,512]{2,1,0:T(8,128)S(1)}, f32[2,256,512]{2,1,0:T(8,128)S(1)}, u32[]{:S(2)}, u32[]{:S(2)}) %collective-permute-start.6) | collective-permute-done | bytes 1048608 | tf_op jit(solution)/shard_map/ppermute | solution.py:25
  45.0 1.2 %place.3 = f32[2,2,256,512]{3,2,1,0:T(8,128)} custom-call(s32[2,8,128]{2,1,0:T(8,128)S(1)} %copy-done.3, f32[2,256,512]{2,1,0:T(8,128)S(1)} %collective-permute-done.6.got_ref, f32[2,2,256,512]{3,2,1,0:T(8,128)} %place.2.rest_0_), custom_call_target="tpu_custom_call", output_to_operand_aliasing={{}: (2, {})} | custom-call | tf_op jit(solution)/shard_map/place/pallas_call | solution.py:195
  (17 shorter events, 0.2 us)
Async XLA Ops:
  0.0 1.2 %copy-start = (bf16[2,512,512]{2,1,0:T(8,128)(2,1)S(1)}, bf16[2,512,512]{2,1,0:T(8,128)(2,1)}, u32[]{:S(2)}) copy-start(bf16[2,512,512]{2,1,0:T(8,128)(2,1)} %param.4) | copy-start | bytes 3145732
  0.0 7.2 %copy-start.5 = (s32[2,32]{1,0:T(2,128)S(1)}, s32[2,32]{1,0:T(2,128)}, u32[]{:S(2)}) copy-start(s32[2,32]{1,0:T(2,128)} %param.5) | copy-start | bytes 772
  0.0 13.6 %collective-permute-start = (bf16[2,2,2,512,1024]{4,3,2,1,0:T(8,128)(2,1)}, bf16[2,2,2,512,1024]{4,3,2,1,0:T(8,128)(2,1)}, u32[]{:S(2)}, u32[]{:S(2)}) collective-permute-start(bf16[2,2,2,512,1024]{4,3,2,1,0:T(8,128)(2,1)} %pair_ref.1), channel_id=1, source_target_pairs={{0,1},{1,0},{2,3},{3,2},{4,5},{5,4},{6,7},{7,6},{8,9},{9,8},{10,11... | collective-permute-start | bytes 25165832 | tf_op jit(solution)/shard_map/ppermute | solution.py:25
  1.4 11.8 %collective-permute-start.1 = (bf16[512,256]{1,0:T(8,128)(2,1)S(1)}, bf16[512,256]{1,0:T(8,128)(2,1)S(1)}, u32[]{:S(2)}, u32[]{:S(2)}) collective-permute-start(bf16[512,256]{1,0:T(8,128)(2,1)S(1)} %pad_maximum_fusion), channel_id=1, source_target_pairs={{0,16},{2,18},{4,20},{6,22},{8,0},{10,2},{12,4},{14,6},{16,24},{18... | collective-permute-start | bytes 786440 | tf_op jit(solution)/shard_map/ppermute | solution.py:223
  5.6 14.3 %collective-permute-start.2 = (bf16[512,256]{1,0:T(8,128)(2,1)S(1)}, bf16[512,256]{1,0:T(8,128)(2,1)S(1)}, u32[]{:S(2)}, u32[]{:S(2)}) collective-permute-start(bf16[512,256]{1,0:T(8,128)(2,1)S(1)} %pad_maximum_fusion.1), channel_id=1, source_target_pairs={{0,16},{2,18},{4,20},{6,22},{8,0},{10,2},{12,4},{14,6},{16,24},{18... | collective-permute-start | bytes 786440 | tf_op jit(solution)/shard_map/ppermute | solution.py:223
  8.1 5.6 %copy-start.4 = (s32[2,2]{1,0:T(2,128)S(1)}, s32[2,2]{1,0:T(2,128)}, u32[]{:S(2)}) copy-start(s32[2,2]{1,0:T(2,128)} %broadcast_select_fusion.users.rest_0_) | copy-start | bytes 52
  13.6 1.6 %copy-start.1 = (bf16[2,512,1024]{2,1,0:T(8,128)(2,1)S(1)}, bf16[2,512,1024]{2,1,0:T(8,128)(2,1)}, u32[]{:S(2)}) copy-start(bf16[2,512,1024]{2,1,0:T(8,128)(2,1)} %get-tuple-element.16.rest_1_) | copy-start | bytes 6291460
  19.8 14.7 %copy-start.2 = (bf16[2,512,1024]{2,1,0:T(8,128)(2,1)S(1)}, bf16[2,512,1024]{2,1,0:T(8,128)(2,1)}, u32[]{:S(2)}) copy-start(bf16[2,512,1024]{2,1,0:T(8,128)(2,1)} %get-tuple-element.15.rest_1_.rest_0_) | copy-start | bytes 6291460
  23.2 11.3 %collective-permute-start.5 = (f32[2,512,512]{2,1,0:T(8,128)S(1)}, f32[2,512,512]{2,1,0:T(8,128)S(1)}, u32[]{:S(2)}, u32[]{:S(2)}) collective-permute-start(f32[2,512,512]{2,1,0:T(8,128)S(1)} %get-tuple-element.20.rest_4_), channel_id=1, source_target_pairs={{0,1},{1,0},{2,3},{3,2},{4,5},{5,4},{6,7},{7,6},{8,9},{9,8},{10,11... | collective-permute-start | bytes 6291464 | tf_op jit(solution)/shard_map/ppermute | solution.py:25
  23.6 10.9 %collective-permute-start.4 = (bf16[512,256]{1,0:T(8,128)(2,1)S(1)}, bf16[512,256]{1,0:T(8,128)(2,1)S(1)}, u32[]{:S(2)}, u32[]{:S(2)}) collective-permute-start(bf16[512,256]{1,0:T(8,128)(2,1)S(1)} %pad_maximum_fusion), channel_id=1, source_target_pairs={{0,8},{2,10},{4,12},{6,14},{8,24},{10,26},{12,28},{14,30},{16,0},{... | collective-permute-start | bytes 786440 | tf_op jit(solution)/shard_map/ppermute | solution.py:223
  26.3 13.5 %collective-permute-start.3 = (bf16[512,256]{1,0:T(8,128)(2,1)S(1)}, bf16[512,256]{1,0:T(8,128)(2,1)S(1)}, u32[]{:S(2)}, u32[]{:S(2)}) collective-permute-start(bf16[512,256]{1,0:T(8,128)(2,1)S(1)} %pad_maximum_fusion.1), channel_id=1, source_target_pairs={{0,8},{2,10},{4,12},{6,14},{8,24},{10,26},{12,28},{14,30},{16,0},{... | collective-permute-start | bytes 786440 | tf_op jit(solution)/shard_map/ppermute | solution.py:223
  37.5 4.9 %copy-start.3 = (s32[2,8,128]{2,1,0:T(8,128)S(1)}, s32[2,8,128]{2,1,0:T(8,128)}, u32[]{:S(2)}) copy-start(s32[2,8,128]{2,1,0:T(8,128)} %get-tuple-element.14.slot_ref) | copy-start | bytes 24580
  42.3 2.7 %collective-permute-start.6 = (f32[2,256,512]{2,1,0:T(8,128)S(1)}, f32[2,256,512]{2,1,0:T(8,128)S(1)}, u32[]{:S(2)}, u32[]{:S(2)}) collective-permute-start(f32[2,256,512]{2,1,0:T(8,128)S(1)} %get-tuple-element.21), channel_id=1, source_target_pairs={{0,1},{1,0},{2,3},{3,2},{4,5},{5,4},{6,7},{7,6},{8,9},{9,8},{10,11... | collective-permute-start | bytes 3145736 | tf_op jit(solution)/shard_map/ppermute | solution.py:25

commit v3 on v2

--- a/solution.py
+++ b/solution.py
@@ -11,7 +11,7 @@
 ROUNDS = 2
 PARTS = 2
 VMEM_LIMIT = 12 << 20
-STAGE_LIMIT = 55 << 20
+STAGE_LIMIT = 44 << 20
 SMEM = pl.BlockSpec(memory_space=pltpu.SMEM)
 VMEM = pl.BlockSpec(memory_space=pltpu.VMEM)
 HBM = pl.BlockSpec(memory_space=pltpu.HBM)
@@ -70,6 +70,36 @@
     )(users, pair_tensors)
 
 
+def hand_out(total, keep_ref, send_ref):
+    rows = keep_ref.shape[0]
+    flip = lax.axis_index("aux") == 0
+    keep_ref[...] = jnp.where(flip, total[:rows], total[rows:])
+    send_ref[...] = jnp.where(flip, total[rows:], total[:rows])
+
+
+def imag_kernel(left_ref, source_ref, keep_ref, send_ref, *, factor):
+    total = lax.dot_general(
+        left_ref[1], left_ref[0], (((1,), (1,)), ((), ())), preferred_element_type=jnp.float32
+    )
+    hand_out(source_ref[1] + total * factor, keep_ref, send_ref)
+
+
+def add_imag(left, source, factor):
+    nao = left.shape[1]
+    rows_shape = jax.ShapeDtypeStruct((nao // 2, nao), jnp.float32)
+    return pl.pallas_call(
+        functools.partial(imag_kernel, factor=factor),
+        out_shape=(rows_shape,) * 2,
+        in_specs=[VMEM] * 2,
+        out_specs=(VMEM,) * 2,
+        compiler_params=pltpu.CompilerParams(vmem_limit_bytes=VMEM_LIMIT),
+        cost_estimate=pl.CostEstimate(
+            flops=2 * nao * nao * left.shape[2], transcendentals=0, bytes_accessed=2 << 20
+        ),
+        name="add_imag",
+    )(left, source)
+
+
 def term_kernel(*rest, factor, wave, part, fetch, earlier, blocks):
     users = None
     if not (wave and part):
@@ -81,7 +111,7 @@
         if part:
             full_ref, sources = sources[-1], sources[:-1]
     elif wave and part:
-        out_ref, send_ref, block_ref, left_ref = rest
+        out_ref, send_ref, left_ref, block_ref = rest
     else:
         out_ref, block_ref, left_ref = rest
     nao, width = mine_ref.shape
@@ -112,7 +142,7 @@
         left_ref[1, :, at + occupied : at + width] = -half[:, :occupied]
     if len(sources) == 2:
         same = users[wave - 1, core] == users[wave, core]
-    for kind in range(2):
+    for kind in range(1 if wave and part else 2):
         total = lax.dot_general(
             left_ref[kind], left_ref[0], (((1,), (1,)), ((), ())), preferred_element_type=jnp.float32
         )
@@ -122,10 +152,7 @@
         if len(sources) == 2:
             total = jnp.where(same, sources[0][kind], sources[1][kind]) + total
         if wave and part:
-            rows = out_ref.shape[1]
-            flip = core == 0
-            out_ref[kind] = jnp.where(flip, total[:rows], total[rows:])
-            send_ref[kind] = jnp.where(flip, total[rows:], total[:rows])
+            hand_out(total, out_ref, send_ref)
         else:
             out_ref[kind] = total
     if fetch is not None and fetch != wave:
@@ -136,7 +163,7 @@
     nao, width = mine.shape
     funcs = own.shape[0]
     whole = jax.ShapeDtypeStruct((2, nao, nao), jnp.float32)
-    rows_shape = jax.ShapeDtypeStruct((2, nao // 2, nao), jnp.float32)
+    rows_shape = jax.ShapeDtypeStruct((nao // 2, nao), jnp.float32)
     pair_shape = jax.ShapeDtypeStruct(own.shape, own.dtype)
     fetch = {(0, 0): 0, (0, 1): 1}.get((wave, part))
     scratch = [
@@ -144,7 +171,11 @@
         pltpu.VMEM((2, nao, 2 * funcs * width), jnp.bfloat16),
     ]
     if fetch is None:
-        out_shape = (rows_shape, rows_shape) if part else (whole,)
+        out_shape = (whole,)
+        if part:
+            left_shape = jax.ShapeDtypeStruct((2, nao, 2 * funcs * width), jnp.bfloat16)
+            out_shape = (rows_shape, rows_shape, left_shape)
+            scratch.pop()
     else:
         out_shape = (whole, pair_shape)
         scratch.append(pltpu.SemaphoreType.DMA)
@@ -176,28 +207,31 @@
     )(*operands)
 
 
-def place_kernel(slot_ref, got_ref, *rest, side):
-    out_ref, sem = rest[-2:]
+def place_kernel(slot_ref, real_ref, imag_ref, *rest, side):
+    out_ref, sems = rest[-2:]
     spot = jnp.max(slot_ref[side])
-    store = pltpu.make_async_copy(got_ref, out_ref.at[spot], sem)
-    store.start()
-    store.wait()
+    stores = []
+    for kind, got_ref in enumerate((real_ref, imag_ref)):
+        stores.append(pltpu.make_async_copy(got_ref, out_ref.at[spot, kind], sems.at[kind]))
+        stores[-1].start()
+    for store in stores:
+        store.wait()
 
 
 def place(slots, got, partial_out, per_device):
-    operands = [slots, got]
-    in_specs = [VMEM, VMEM]
+    operands = [slots, *got]
+    in_specs = [VMEM] * 3
     aliases = {}
     if partial_out is not None:
         operands.append(partial_out)
         in_specs.append(HBM)
-        aliases = {2: 0}
+        aliases = {3: 0}
     return pl.pallas_call(
         functools.partial(place_kernel, side=len(aliases)),
-        out_shape=jax.ShapeDtypeStruct((per_device,) + got.shape, got.dtype),
+        out_shape=jax.ShapeDtypeStruct((per_device, 2) + got[0].shape, jnp.float32),
         in_specs=in_specs,
         out_specs=HBM,
-        scratch_shapes=[pltpu.SemaphoreType.DMA],
+        scratch_shapes=[pltpu.SemaphoreType.DMA((2,))],
         input_output_aliases=aliases,
         compiler_params=pltpu.CompilerParams(vmem_limit_bytes=VMEM_LIMIT),
         name="place",
@@ -231,6 +265,7 @@
     sources = []
     near = None
     for wave, part, mine in arrived:
+        before = sources[0] if sources else None
         got = add_terms(users, own[wave], near, mine, sources, sib, factor, wave, part, blocks)
         if wave == 0 and part == 0:
             near = got[1]
@@ -238,9 +273,12 @@
         if wave == 0 and part == PARTS - 1:
             near = got[1]
             sources = [got[0], from_sibling(got[0])]
-    received = from_sibling(got[1])
-    kept = place(slots, got[0], None, per_device)
-    return place(slots, received, kept, per_device)
+    keep_real, send_real, left = got
+    real = from_sibling(send_real)
+    keep_imag, send_imag = add_imag(left, before, factor)
+    imag = from_sibling(send_imag)
+    kept = place(slots, (keep_real, keep_imag), None, per_device)
+    return place(slots, (real, imag), kept, per_device)
 
 
 def build_block(chosen):

time: 46.5 us -> 44.9 us (0.966)
  waiting for transfers between devices: 9.79 us -> 12.2 us
  Pallas kernels: 20.8 us -> 18.7 us
  local copies, waits for them, and re-layouts: 2.49 us -> 0.89 us
  other arithmetic: 0.87 us -> 0.29 us
  starting transfers between devices: 12 us -> 12.5 us
    pallas_call x1, Pallas kernels: 5.1 us -> 2.82 us  [stage(): pl.pallas_call(functools.partial(stage_kernel, blocks=blocks), out_shape=...]
    ppermute x4, waiting for transfers between devices: 7.9 us -> 9.8 us  [paired_body(): arrived.append((wave, part, lax.ppermute(chunk, 'kpt', targets)))]
    unnamed x12 -> x4, local copies, waits for them, and re-layouts: 2.34 us -> 0.73 us
    pallas_call x0 -> x1, Pallas kernels: none -> 0.77 us  [add_imag(): pl.pallas_call(functools.partial(imag_kernel, factor=factor), out_shape=(...]
    pallas_call x4, Pallas kernels: 13.4 us -> 12.7 us  [add_terms(): pl.pallas_call(kernel, out_shape=out_shape, in_specs=in_specs, out_specs=...]
    select_n x1, other arithmetic: 0.58 us -> 0.01 us  [paired_body(): users = jnp.where(first_round == 0, users, users[::-1])]
    ppermute x3 -> x4, starting transfers between devices: 1 us -> 1.5 us  [from_sibling(): return lax.ppermute(shard, 'aux', [(0, 1), (1, 0)])]
    ppermute x3 -> x4, waiting for transfers between devices: 1.89 us -> 2.38 us  [from_sibling(): return lax.ppermute(shard, 'aux', [(0, 1), (1, 0)])]
  transfers between devices with their start and end apart: 7 -> 8, of which waited for: 4 -> 6; matrix products, arithmetic and copies ran while one was open for 2% -> 1% of each run, Pallas kernels for 30% -> 26%
where the time goes in v3:
time: 44.9 us; the launch traced here: 44.7 us
  Pallas kernels  18.7 us (42%)
  starting transfers between devices  12.5 us (28%)
  waiting for transfers between devices  12.2 us (27%)
  local copies, waits for them, and re-layouts  0.89 us (2%)
    pallas_call x4, Pallas kernels, add_terms(): pl.pallas_call(kernel, out_shape=out_shape, in_specs=in_specs, out_specs=...  12.7 us
    ppermute x4, starting transfers between devices, paired_body(): arrived.append((wave, part, lax.ppermute(chunk, 'kpt', targets)))  11 us
    ppermute x4, waiting for transfers between devices, paired_body(): arrived.append((wave, part, lax.ppermute(chunk, 'kpt', targets)))  9.8 us
    pallas_call x1, Pallas kernels, stage(): pl.pallas_call(functools.partial(stage_kernel, blocks=blocks), out_shape=...  2.82 us
    ppermute x4, waiting for transfers between devices, from_sibling(): return lax.ppermute(shard, 'aux', [(0, 1), (1, 0)])  2.38 us
    pallas_call x2, Pallas kernels, place(): pl.pallas_call(functools.partial(place_kernel, side=len(aliases)), out_sh...  2.35 us
    ppermute x4, starting transfers between devices, from_sibling(): return lax.ppermute(shard, 'aux', [(0, 1), (1, 0)])  1.5 us
  transfers between devices with their start and end apart: 8, of which 6 were waited for; matrix products, arithmetic and copies ran while one was open for 1% of the time, Pallas kernels for 26%

profile of v3, /device:TPU:0, one launch (start us, length us, event | category | flops | bytes accessed | tf_op | source)
XLA Modules:
  0.0 44.7 jit_solution(3394046184476102802)
XLA Ops:
  0.0 0.5 %collective-permute-start = (bf16[2,2,2,512,1024]{4,3,2,1,0:T(8,128)(2,1)}, bf16[2,2,2,512,1024]{4,3,2,1,0:T(8,128)(2,1)}, u32[]{:S(2)}, u32[]{:S(2)}) collective-permute-start(bf16[2,2,2,512,1024]{4,3,2,1,0:T(8,128)(2,1)} %pair_ref.1), channel_id=1, source_target_pairs={{0,1},{1,0},{2,3},{3,2},{4,5},{5,4},{6,7},{7,6},{8,9},{9,8},{10,11... | collective-permute-start | bytes 25165832 | tf_op jit(solution)/shard_map/ppermute | solution.py:25
  0.5 0.7 %copy-done = bf16[2,512,512]{2,1,0:T(8,128)(2,1)S(1)} copy-done((bf16[2,512,512]{2,1,0:T(8,128)(2,1)S(1)}, bf16[2,512,512]{2,1,0:T(8,128)(2,1)}, u32[]{:S(2)}) %copy-start) | copy-done | bytes 1048600
  1.3 0.1 fusion.2
  1.4 4.1 %collective-permute-start.1 = (bf16[512,256]{1,0:T(8,128)(2,1)S(1)}, bf16[512,256]{1,0:T(8,128)(2,1)S(1)}, u32[]{:S(2)}, u32[]{:S(2)}) collective-permute-start(bf16[512,256]{1,0:T(8,128)(2,1)S(1)} %pad_maximum_fusion), channel_id=1, source_target_pairs={{0,16},{2,18},{4,20},{6,22},{8,0},{10,2},{12,4},{14,6},{16,24},{18... | collective-permute-start | bytes 786440 | tf_op jit(solution)/shard_map/ppermute | solution.py:257
  5.6 1.6 %collective-permute-start.2 = (bf16[512,256]{1,0:T(8,128)(2,1)S(1)}, bf16[512,256]{1,0:T(8,128)(2,1)S(1)}, u32[]{:S(2)}, u32[]{:S(2)}) collective-permute-start(bf16[512,256]{1,0:T(8,128)(2,1)S(1)} %pad_maximum_fusion.1), channel_id=1, source_target_pairs={{0,16},{2,18},{4,20},{6,22},{8,0},{10,2},{12,4},{14,6},{16,24},{18... | collective-permute-start | bytes 786440 | tf_op jit(solution)/shard_map/ppermute | solution.py:257
  7.3 0.1 fusion
  7.5 2.8 %stage.1 = (bf16[2,512,1024]{2,1,0:T(8,128)(2,1)S(1)}, bf16[2,512,1024]{2,1,0:T(8,128)(2,1)S(1)}, s32[2,8,128]{2,1,0:T(8,128)S(1)}) custom-call(s32[2,2]{1,0:T(2,128)S(1)} %broadcast_select_fusion.users.rest_0_, bf16[2,2,2,512,1024]{4,3,2,1,0:T(8,128)(2,1)} %pair_ref.1), custom_call_target="tpu_custom_call" | custom-call | tf_op jit(solution)/shard_map/stage/pallas_call | solution.py:62
  10.3 1.9 %collective-permute-done.1.rest_3_ = bf16[512,256]{1,0:T(8,128)(2,1)S(1)} collective-permute-done((bf16[512,256]{1,0:T(8,128)(2,1)S(1)}, bf16[512,256]{1,0:T(8,128)(2,1)S(1)}, u32[]{:S(2)}, u32[]{:S(2)}) %collective-permute-start.1) | collective-permute-done | bytes 262176 | tf_op jit(solution)/shard_map/ppermute | solution.py:257
  12.2 1.4 %collective-permute-done.rest_2_.rest_5_ = bf16[2,2,2,512,1024]{4,3,2,1,0:T(8,128)(2,1)} collective-permute-done((bf16[2,2,2,512,1024]{4,3,2,1,0:T(8,128)(2,1)}, bf16[2,2,2,512,1024]{4,3,2,1,0:T(8,128)(2,1)}, u32[]{:S(2)}, u32[]{:S(2)}) %collective-permute-start) | collective-permute-done | bytes 8388640 | tf_op jit(solution)/shard_map/ppermute | solution.py:25
  13.6 4.6 %shard_map.37 = (f32[2,512,512]{2,1,0:T(8,128)S(1)}, bf16[2,512,1024]{2,1,0:T(8,128)(2,1)S(1)}) custom-call(s32[2,2]{1,0:T(2,128)S(1)} %broadcast_select_fusion.users.rest_0_, bf16[2,512,1024]{2,1,0:T(8,128)(2,1)S(1)} %get-tuple-element.19.rest_1_, bf16[2,2,2,512,1024]{4,3,2,1,0:T(8,128)(2,1)} %collective-permute-done.rest_2_.rest_5_, ...), custom_call_target="tpu_custom_call" | custom-call | flops 2147483648 | bytes 6291456 | tf_op jit(solution)/shard_map/pallas_call | solution.py:199
  18.2 3.3 %shard_map.38 = (f32[2,512,512]{2,1,0:T(8,128)S(1)}, bf16[2,512,1024]{2,1,0:T(8,128)(2,1)S(1)}) custom-call(s32[2,2]{1,0:T(2,128)S(1)} %broadcast_select_fusion.users.rest_0_, bf16[2,512,1024]{2,1,0:T(8,128)(2,1)S(1)} %get-tuple-element.19.rest_1_, bf16[2,512,1024]{2,1,0:T(8,128)(2,1)S(1)} %get-tuple-element.20.rest_2_, ...), custom_call_target="tpu_custom_call" | custom-call | flops 2147483648 | bytes 6291456 | tf_op jit(solution)/shard_map/pallas_call | solution.py:199
  21.6 0.4 collective-permute-start.5
  22.0 2.7 %collective-permute-start.4 = (bf16[512,256]{1,0:T(8,128)(2,1)S(1)}, bf16[512,256]{1,0:T(8,128)(2,1)S(1)}, u32[]{:S(2)}, u32[]{:S(2)}) collective-permute-start(bf16[512,256]{1,0:T(8,128)(2,1)S(1)} %pad_maximum_fusion), channel_id=1, source_target_pairs={{0,8},{2,10},{4,12},{6,14},{8,24},{10,26},{12,28},{14,30},{16,0},{... | collective-permute-start | bytes 786440 | tf_op jit(solution)/shard_map/ppermute | solution.py:257
  24.7 2.6 %collective-permute-start.3 = (bf16[512,256]{1,0:T(8,128)(2,1)S(1)}, bf16[512,256]{1,0:T(8,128)(2,1)S(1)}, u32[]{:S(2)}, u32[]{:S(2)}) collective-permute-start(bf16[512,256]{1,0:T(8,128)(2,1)S(1)} %pad_maximum_fusion.1), channel_id=1, source_target_pairs={{0,8},{2,10},{4,12},{6,14},{8,24},{10,26},{12,28},{14,30},{16,0},{... | collective-permute-start | bytes 786440 | tf_op jit(solution)/shard_map/ppermute | solution.py:257
  27.3 5.6 %collective-permute-done.4.rest_3_ = bf16[512,256]{1,0:T(8,128)(2,1)S(1)} collective-permute-done((bf16[512,256]{1,0:T(8,128)(2,1)S(1)}, bf16[512,256]{1,0:T(8,128)(2,1)S(1)}, u32[]{:S(2)}, u32[]{:S(2)}) %collective-permute-start.4) | collective-permute-done | bytes 262176 | tf_op jit(solution)/shard_map/ppermute | solution.py:257
  32.9 3.0 %shard_map.39.rest_3_.source_ref = f32[2,512,512]{2,1,0:T(8,128)S(1)} custom-call(s32[2,2]{1,0:T(2,128)S(1)} %broadcast_select_fusion.users.rest_0_, bf16[2,512,1024]{2,1,0:T(8,128)(2,1)S(1)} %get-tuple-element.18.rest_1_.rest_0_, bf16[2,512,1024]{2,1,0:T(8,128)(2,1)S(1)} %get-tuple-element.22.rest_2_.rest_1_, ...), custom_call_target="tpu_custom_call" | custom-call | flops 2147483648 | bytes 6291456 | tf_op jit(solution)/shard_map/pallas_call | solution.py:199
  35.8 2.3 %collective-permute-done.3.rest_2_ = bf16[512,256]{1,0:T(8,128)(2,1)S(1)} collective-permute-done((bf16[512,256]{1,0:T(8,128)(2,1)S(1)}, bf16[512,256]{1,0:T(8,128)(2,1)S(1)}, u32[]{:S(2)}, u32[]{:S(2)}) %collective-permute-start.3) | collective-permute-done | bytes 262176 | tf_op jit(solution)/shard_map/ppermute | solution.py:257
  38.2 1.9 %shard_map.40 = (f32[256,512]{1,0:T(8,128)S(1)}, f32[256,512]{1,0:T(8,128)S(1)}, bf16[2,512,1024]{2,1,0:T(8,128)(2,1)S(1)}) custom-call(bf16[2,512,1024]{2,1,0:T(8,128)(2,1)S(1)} %get-tuple-element.18.rest_1_.rest_0_, bf16[2,512,1024]{2,1,0:T(8,128)(2,1)S(1)} %get-tuple-element.22.rest_2_.rest_1_, bf16[512,256]{1,0:T(8,128)(2,1)S(1)} %collective-permute-done.3.rest_2_, ...), custom_call_target="tpu_custom_call" | custom-call | flops 2147483648 | bytes 6291456 | tf_op jit(solution)/shard_map/pallas_call | solution.py:199
  40.0 0.8 %add_imag.1 = (f32[256,512]{1,0:T(8,128)S(1)}, f32[256,512]{1,0:T(8,128)S(1)}) custom-call(bf16[2,512,1024]{2,1,0:T(8,128)(2,1)S(1)} %get-tuple-element.25.left_ref, f32[2,512,512]{2,1,0:T(8,128)S(1)} %shard_map.39.rest_3_.source_ref), custom_call_target="tpu_custom_call" | custom-call | flops 536870912 | bytes 2097152 | tf_op jit(solution)/shard_map/add_imag/pallas_call | solution.py:90
  40.9 0.5 %collective-permute-start.6 = (f32[256,512]{1,0:T(8,128)S(1)}, f32[256,512]{1,0:T(8,128)S(1)}, u32[]{:S(2)}, u32[]{:S(2)}) collective-permute-start(f32[256,512]{1,0:T(8,128)S(1)} %get-tuple-element.24), channel_id=1, source_target_pairs={{0,1},{1,0},{2,3},{3,2},{4,5},{5,4},{6,7},{7,6},{8,9},{9,8},{10,11... | collective-permute-start | bytes 1572872 | tf_op jit(solution)/shard_map/ppermute | solution.py:25
  41.4 1.2 %place.2.rest_0_ = f32[2,2,256,512]{3,2,1,0:T(8,128)} custom-call(s32[2,8,128]{2,1,0:T(8,128)S(1)} %get-tuple-element.17.slot_ref, f32[256,512]{1,0:T(8,128)S(1)} %get-tuple-element.27.real_ref, f32[256,512]{1,0:T(8,128)S(1)} %get-tuple-element.28.imag_ref), custom_call_target="tpu_custom_call" | custom-call | tf_op jit(solution)/shard_map/place/pallas_call | solution.py:229
  42.6 0.2 collective-permute-done.7.imag_ref
  42.8 0.7 %collective-permute-done.6.real_ref = f32[256,512]{1,0:T(8,128)S(1)} collective-permute-done((f32[256,512]{1,0:T(8,128)S(1)}, f32[256,512]{1,0:T(8,128)S(1)}, u32[]{:S(2)}, u32[]{:S(2)}) %collective-permute-start.6) | collective-permute-done | bytes 524320 | tf_op jit(solution)/shard_map/ppermute | solution.py:25
  43.5 1.2 %place.3 = f32[2,2,256,512]{3,2,1,0:T(8,128)} custom-call(s32[2,8,128]{2,1,0:T(8,128)S(1)} %get-tuple-element.17.slot_ref, f32[256,512]{1,0:T(8,128)S(1)} %collective-permute-done.6.real_ref, f32[256,512]{1,0:T(8,128)S(1)} %collective-permute-done.7.imag_ref, f32[2,2,256,512]{3,2,1,0:T(8,128)} %place.2.rest_0_), custom_call_target="tpu_custom_call", output_to_operand_aliasing={{}: (3, {})} | custom-call | tf_op jit(solution)/shard_map/place/pallas_call | solution.py:229
  (12 shorter events, 0.3 us)
Async XLA Ops:
  0.0 1.2 %copy-start = (bf16[2,512,512]{2,1,0:T(8,128)(2,1)S(1)}, bf16[2,512,512]{2,1,0:T(8,128)(2,1)}, u32[]{:S(2)}) copy-start(bf16[2,512,512]{2,1,0:T(8,128)(2,1)} %param.4) | copy-start | bytes 3145732
  0.0 7.2 %copy-start.1 = (s32[2,32]{1,0:T(2,128)S(1)}, s32[2,32]{1,0:T(2,128)}, u32[]{:S(2)}) copy-start(s32[2,32]{1,0:T(2,128)} %param.5) | copy-start | bytes 772
  0.0 13.6 %collective-permute-start = (bf16[2,2,2,512,1024]{4,3,2,1,0:T(8,128)(2,1)}, bf16[2,2,2,512,1024]{4,3,2,1,0:T(8,128)(2,1)}, u32[]{:S(2)}, u32[]{:S(2)}) collective-permute-start(bf16[2,2,2,512,1024]{4,3,2,1,0:T(8,128)(2,1)} %pair_ref.1), channel_id=1, source_target_pairs={{0,1},{1,0},{2,3},{3,2},{4,5},{5,4},{6,7},{7,6},{8,9},{9,8},{10,11... | collective-permute-start | bytes 25165832 | tf_op jit(solution)/shard_map/ppermute | solution.py:25
  1.4 10.8 %collective-permute-start.1 = (bf16[512,256]{1,0:T(8,128)(2,1)S(1)}, bf16[512,256]{1,0:T(8,128)(2,1)S(1)}, u32[]{:S(2)}, u32[]{:S(2)}) collective-permute-start(bf16[512,256]{1,0:T(8,128)(2,1)S(1)} %pad_maximum_fusion), channel_id=1, source_target_pairs={{0,16},{2,18},{4,20},{6,22},{8,0},{10,2},{12,4},{14,6},{16,24},{18... | collective-permute-start | bytes 786440 | tf_op jit(solution)/shard_map/ppermute | solution.py:257
  5.6 12.7 %collective-permute-start.2 = (bf16[512,256]{1,0:T(8,128)(2,1)S(1)}, bf16[512,256]{1,0:T(8,128)(2,1)S(1)}, u32[]{:S(2)}, u32[]{:S(2)}) collective-permute-start(bf16[512,256]{1,0:T(8,128)(2,1)S(1)} %pad_maximum_fusion.1), channel_id=1, source_target_pairs={{0,16},{2,18},{4,20},{6,22},{8,0},{10,2},{12,4},{14,6},{16,24},{18... | collective-permute-start | bytes 786440 | tf_op jit(solution)/shard_map/ppermute | solution.py:257
  21.6 11.3 %collective-permute-start.5 = (f32[2,512,512]{2,1,0:T(8,128)S(1)}, f32[2,512,512]{2,1,0:T(8,128)S(1)}, u32[]{:S(2)}, u32[]{:S(2)}) collective-permute-start(f32[2,512,512]{2,1,0:T(8,128)S(1)} %get-tuple-element.23.rest_4_), channel_id=1, source_target_pairs={{0,1},{1,0},{2,3},{3,2},{4,5},{5,4},{6,7},{7,6},{8,9},{9,8},{10,11... | collective-permute-start | bytes 6291464 | tf_op jit(solution)/shard_map/ppermute | solution.py:25
  22.0 10.9 %collective-permute-start.4 = (bf16[512,256]{1,0:T(8,128)(2,1)S(1)}, bf16[512,256]{1,0:T(8,128)(2,1)S(1)}, u32[]{:S(2)}, u32[]{:S(2)}) collective-permute-start(bf16[512,256]{1,0:T(8,128)(2,1)S(1)} %pad_maximum_fusion), channel_id=1, source_target_pairs={{0,8},{2,10},{4,12},{6,14},{8,24},{10,26},{12,28},{14,30},{16,0},{... | collective-permute-start | bytes 786440 | tf_op jit(solution)/shard_map/ppermute | solution.py:257
  24.7 13.5 %collective-permute-start.3 = (bf16[512,256]{1,0:T(8,128)(2,1)S(1)}, bf16[512,256]{1,0:T(8,128)(2,1)S(1)}, u32[]{:S(2)}, u32[]{:S(2)}) collective-permute-start(bf16[512,256]{1,0:T(8,128)(2,1)S(1)} %pad_maximum_fusion.1), channel_id=1, source_target_pairs={{0,8},{2,10},{4,12},{6,14},{8,24},{10,26},{12,28},{14,30},{16,0},{... | collective-permute-start | bytes 786440 | tf_op jit(solution)/shard_map/ppermute | solution.py:257
  40.8 2.0 %collective-permute-start.7 = (f32[256,512]{1,0:T(8,128)S(1)}, f32[256,512]{1,0:T(8,128)S(1)}, u32[]{:S(2)}, u32[]{:S(2)}) collective-permute-start(f32[256,512]{1,0:T(8,128)S(1)} %get-tuple-element.26), channel_id=1, source_target_pairs={{0,1},{1,0},{2,3},{3,2},{4,5},{5,4},{6,7},{7,6},{8,9},{9,8},{10,11... | collective-permute-start | bytes 1572872 | tf_op jit(solution)/shard_map/ppermute | solution.py:25
  40.9 2.6 %collective-permute-start.6 = (f32[256,512]{1,0:T(8,128)S(1)}, f32[256,512]{1,0:T(8,128)S(1)}, u32[]{:S(2)}, u32[]{:S(2)}) collective-permute-start(f32[256,512]{1,0:T(8,128)S(1)} %get-tuple-element.24), channel_id=1, source_target_pairs={{0,1},{1,0},{2,3},{3,2},{4,5},{5,4},{6,7},{7,6},{8,9},{9,8},{10,11... | collective-permute-start | bytes 1572872 | tf_op jit(solution)/shard_map/ppermute | solution.py:25

commit v4 on v3

--- a/solution.py
+++ b/solution.py
@@ -9,7 +9,7 @@
 
 
 ROUNDS = 2
-PARTS = 2
+PARTS = ((2, 2), (2, 1, 1))
 VMEM_LIMIT = 12 << 20
 STAGE_LIMIT = 44 << 20
 SMEM = pl.BlockSpec(memory_space=pltpu.SMEM)
@@ -52,13 +52,15 @@
         loads[-1].start()
     for side, at in enumerate((core, 1 - core)):
         slot_ref[side] = jnp.full(slot_ref.shape[1:], users[ROUNDS - 1, at], jnp.int32)
+    same = (users[0, core] == users[ROUNDS - 1, core]).astype(jnp.int32)
+    slot_ref[2] = jnp.full(slot_ref.shape[1:], same, jnp.int32)
     for load in loads:
         load.wait()
 
 
 def stage(users, pair_tensors, blocks):
     shape = jax.ShapeDtypeStruct(pair_tensors.shape[2:], pair_tensors.dtype)
-    slots = jax.ShapeDtypeStruct((2, 8, 128), jnp.int32)
+    slots = jax.ShapeDtypeStruct((3, 8, 128), jnp.int32)
     return pl.pallas_call(
         functools.partial(stage_kernel, blocks=blocks),
         out_shape=(shape,) * ROUNDS + (slots,),
@@ -82,6 +84,22 @@
         left_ref[1], left_ref[0], (((1,), (1,)), ((), ())), preferred_element_type=jnp.float32
     )
     hand_out(source_ref[1] + total * factor, keep_ref, send_ref)
+
+
+def fold_kernel(slot_ref, sums_ref, own_ref, other_ref, out_ref):
+    same = jnp.max(slot_ref[2]) > 0
+    out_ref[...] = sums_ref[...] + jnp.where(same, own_ref[...], other_ref[...])
+
+
+def fold(slots, sums, own, other):
+    return pl.pallas_call(
+        fold_kernel,
+        out_shape=jax.ShapeDtypeStruct(sums.shape, sums.dtype),
+        in_specs=[VMEM] * 4,
+        out_specs=VMEM,
+        compiler_params=pltpu.CompilerParams(vmem_limit_bytes=VMEM_LIMIT),
+        name="fold",
+    )(slots, sums, own, other)
 
 
 def add_imag(left, source, factor):
@@ -100,9 +118,9 @@
     )(left, source)
 
 
-def term_kernel(*rest, factor, wave, part, fetch, earlier, blocks):
+def term_kernel(*rest, factor, wave, part, last, fetch, earlier, blocks):
     users = None
-    if not (wave and part):
+    if fetch is not None:
         users, *rest = rest
     own_ref, sib_ref, mine_ref, *rest = rest
     sources, rest = rest[:earlier], rest[earlier:]
@@ -110,7 +128,7 @@
         full_ref, out_ref, got_ref, block_ref, left_ref, sem = (sib_ref, *rest)
         if part:
             full_ref, sources = sources[-1], sources[:-1]
-    elif wave and part:
+    elif last:
         out_ref, send_ref, left_ref, block_ref = rest
     else:
         out_ref, block_ref, left_ref = rest
@@ -140,18 +158,14 @@
         left_ref[0, :, at : at + width] = half
         left_ref[1, :, at : at + occupied] = half[:, occupied:]
         left_ref[1, :, at + occupied : at + width] = -half[:, :occupied]
-    if len(sources) == 2:
-        same = users[wave - 1, core] == users[wave, core]
-    for kind in range(1 if wave and part else 2):
+    for kind in range(1 if last else 2):
         total = lax.dot_general(
             left_ref[kind], left_ref[0], (((1,), (1,)), ((), ())), preferred_element_type=jnp.float32
         )
         total = total * factor
         if len(sources) == 1:
             total = sources[0][kind] + total
-        if len(sources) == 2:
-            total = jnp.where(same, sources[0][kind], sources[1][kind]) + total
-        if wave and part:
+        if last:
             hand_out(total, out_ref, send_ref)
         else:
             out_ref[kind] = total
@@ -166,13 +180,14 @@
     rows_shape = jax.ShapeDtypeStruct((nao // 2, nao), jnp.float32)
     pair_shape = jax.ShapeDtypeStruct(own.shape, own.dtype)
     fetch = {(0, 0): 0, (0, 1): 1}.get((wave, part))
+    last = wave == 1 and part == len(PARTS[1]) - 1
     scratch = [
         pltpu.VMEM((2 * nao, width), jnp.bfloat16),
         pltpu.VMEM((2, nao, 2 * funcs * width), jnp.bfloat16),
     ]
     if fetch is None:
         out_shape = (whole,)
-        if part:
+        if last:
             left_shape = jax.ShapeDtypeStruct((2, nao, 2 * funcs * width), jnp.bfloat16)
             out_shape = (rows_shape, rows_shape, left_shape)
             scratch.pop()
@@ -190,11 +205,12 @@
         factor=factor,
         wave=wave,
         part=part,
+        last=last,
         fetch=fetch,
         earlier=len(operands) - 4,
         blocks=blocks,
     )
-    if fetch is None and part:
+    if fetch is None:
         operands, in_specs = operands[1:], in_specs[1:]
     return pl.pallas_call(
         kernel,
@@ -244,15 +260,17 @@
     blocks = lax.axis_size("kpt")
     factor = 1.0 / (ROUNDS * pair_tensors.shape[2] * lax.axis_size("aux") * occupied) ** 0.5
     offset = lax.axis_index("kpt") * per_device
-    share = occupied // PARTS
     piece = lax.dynamic_index_in_dim(orbitals, lax.axis_index("aux"), 0, keepdims=False)
     sib = from_sibling(pair_tensors)
     arrived = []
     for wave in range(ROUNDS):
         targets = wave_targets(blocks, wave)
-        for part in range(PARTS):
-            real_part = piece[:, part * share : (part + 1) * share]
-            imag_part = piece[:, occupied + part * share : occupied + (part + 1) * share]
+        start = 0
+        for part, weight in enumerate(PARTS[wave]):
+            stop = start + occupied * weight // sum(PARTS[wave])
+            real_part = piece[:, start:stop]
+            imag_part = piece[:, occupied + start : occupied + stop]
+            start = stop
             chunk = jnp.concatenate([real_part, imag_part], axis=1)
             arrived.append((wave, part, lax.ppermute(chunk, "kpt", targets)))
     within = lax.dynamic_slice_in_dim(matchings, offset, per_device, 1) % per_device
@@ -270,9 +288,12 @@
         if wave == 0 and part == 0:
             near = got[1]
         sources = [got[0]]
-        if wave == 0 and part == PARTS - 1:
+        if wave == 0 and part == len(PARTS[0]) - 1:
             near = got[1]
-            sources = [got[0], from_sibling(got[0])]
+            first_sums = [got[0], from_sibling(got[0])]
+            sources = []
+        if wave == 1 and part == len(PARTS[1]) - 2:
+            sources = [fold(slots, sources[0], *first_sums)]
     keep_real, send_real, left = got
     real = from_sibling(send_real)
     keep_imag, send_imag = add_imag(left, before, factor)

time: 44.9 us -> 47 us (1.047)
  Pallas kernels: 18.7 us -> 20.1 us
  starting transfers between devices: 12.5 us -> 13.1 us
    pallas_call x4 -> x5, Pallas kernels: 12.7 us -> 13.9 us  [add_terms(): pl.pallas_call(kernel, out_shape=out_shape, in_specs=in_specs, out_specs=...]
    ppermute x4 -> x5, starting transfers between devices: 11 us -> 11.6 us  [paired_body(): arrived.append((wave, part, lax.ppermute(chunk, 'kpt', targets)))]
    pallas_call x0 -> x1, Pallas kernels: none -> 0.55 us  [fold(): pl.pallas_call(fold_kernel, out_shape=jax.ShapeDtypeStruct(sums.shape, su...]
    ppermute x4 -> x5, waiting for transfers between devices: 9.8 us -> 9.48 us  [paired_body(): arrived.append((wave, part, lax.ppermute(chunk, 'kpt', targets)))]
  transfers between devices with their start and end apart: 8 -> 9, of which waited for: 6 -> 6; matrix products, arithmetic and copies ran while one was open for 1% -> 2% of each run, Pallas kernels for 26% -> 29%
where the time goes in v4:
time: 47 us; the launch traced here: 46.8 us
  Pallas kernels  20.1 us (43%)
  starting transfers between devices  13.1 us (28%)
  waiting for transfers between devices  11.9 us (25%)
  local copies, waits for them, and re-layouts  1.02 us (2%)
  other arithmetic  0.51 us (1%)
    pallas_call x5, Pallas kernels, add_terms(): pl.pallas_call(kernel, out_shape=out_shape, in_specs=in_specs, out_specs=...  13.9 us
    ppermute x5, starting transfers between devices, paired_body(): arrived.append((wave, part, lax.ppermute(chunk, 'kpt', targets)))  11.6 us
    ppermute x5, waiting for transfers between devices, paired_body(): arrived.append((wave, part, lax.ppermute(chunk, 'kpt', targets)))  9.48 us
    pallas_call x1, Pallas kernels, stage(): pl.pallas_call(functools.partial(stage_kernel, blocks=blocks), out_shape=...  2.82 us
    ppermute x4, waiting for transfers between devices, from_sibling(): return lax.ppermute(shard, 'aux', [(0, 1), (1, 0)])  2.38 us
    pallas_call x2, Pallas kernels, place(): pl.pallas_call(functools.partial(place_kernel, side=len(aliases)), out_sh...  2.35 us
    ppermute x4, starting transfers between devices, from_sibling(): return lax.ppermute(shard, 'aux', [(0, 1), (1, 0)])  1.5 us
  transfers between devices with their start and end apart: 9, of which 6 were waited for; matrix products, arithmetic and copies ran while one was open for 2% of the time, Pallas kernels for 29%

profile of v4, /device:TPU:0, one launch (start us, length us, event | category | flops | bytes accessed | tf_op | source)
XLA Modules:
  0.0 46.8 jit_solution(5072345585548931492)
XLA Ops:
  0.0 0.5 %collective-permute-start = (bf16[2,2,2,512,1024]{4,3,2,1,0:T(8,128)(2,1)}, bf16[2,2,2,512,1024]{4,3,2,1,0:T(8,128)(2,1)}, u32[]{:S(2)}, u32[]{:S(2)}) collective-permute-start(bf16[2,2,2,512,1024]{4,3,2,1,0:T(8,128)(2,1)} %pair_ref.1), channel_id=1, source_target_pairs={{0,1},{1,0},{2,3},{3,2},{4,5},{5,4},{6,7},{7,6},{8,9},{9,8},{10,11... | collective-permute-start | bytes 25165832 | tf_op jit(solution)/shard_map/ppermute | solution.py:25
  0.5 0.7 %copy-done = bf16[2,512,512]{2,1,0:T(8,128)(2,1)S(1)} copy-done((bf16[2,512,512]{2,1,0:T(8,128)(2,1)S(1)}, bf16[2,512,512]{2,1,0:T(8,128)(2,1)}, u32[]{:S(2)}) %copy-start) | copy-done | bytes 1048600
  1.4 4.1 %collective-permute-start.1 = (bf16[512,256]{1,0:T(8,128)(2,1)S(1)}, bf16[512,256]{1,0:T(8,128)(2,1)S(1)}, u32[]{:S(2)}, u32[]{:S(2)}) collective-permute-start(bf16[512,256]{1,0:T(8,128)(2,1)S(1)} %pad_maximum_fusion), channel_id=1, source_target_pairs={{0,16},{2,18},{4,20},{6,22},{8,0},{10,2},{12,4},{14,6},{16,24},{18... | collective-permute-start | bytes 786440 | tf_op jit(solution)/shard_map/ppermute | solution.py:275
  5.6 1.6 %collective-permute-start.2 = (bf16[512,256]{1,0:T(8,128)(2,1)S(1)}, bf16[512,256]{1,0:T(8,128)(2,1)S(1)}, u32[]{:S(2)}, u32[]{:S(2)}) collective-permute-start(bf16[512,256]{1,0:T(8,128)(2,1)S(1)} %pad_maximum_fusion.1), channel_id=1, source_target_pairs={{0,16},{2,18},{4,20},{6,22},{8,0},{10,2},{12,4},{14,6},{16,24},{18... | collective-permute-start | bytes 786440 | tf_op jit(solution)/shard_map/ppermute | solution.py:275
  7.5 2.8 %stage.1 = (bf16[2,512,1024]{2,1,0:T(8,128)(2,1)S(1)}, bf16[2,512,1024]{2,1,0:T(8,128)(2,1)S(1)}, s32[3,8,128]{2,1,0:T(8,128)S(1)}) custom-call(s32[2,2]{1,0:T(2,128)S(1)} %broadcast_select_fusion.users.rest_0_, bf16[2,2,2,512,1024]{4,3,2,1,0:T(8,128)(2,1)} %pair_ref.1), custom_call_target="tpu_custom_call" | custom-call | tf_op jit(solution)/shard_map/stage/pallas_call | solution.py:64
  10.3 1.9 %collective-permute-done.1.rest_3_ = bf16[512,256]{1,0:T(8,128)(2,1)S(1)} collective-permute-done((bf16[512,256]{1,0:T(8,128)(2,1)S(1)}, bf16[512,256]{1,0:T(8,128)(2,1)S(1)}, u32[]{:S(2)}, u32[]{:S(2)}) %collective-permute-start.1) | collective-permute-done | bytes 262176 | tf_op jit(solution)/shard_map/ppermute | solution.py:275
  12.2 1.4 %collective-permute-done.rest_2_.rest_5_ = bf16[2,2,2,512,1024]{4,3,2,1,0:T(8,128)(2,1)} collective-permute-done((bf16[2,2,2,512,1024]{4,3,2,1,0:T(8,128)(2,1)}, bf16[2,2,2,512,1024]{4,3,2,1,0:T(8,128)(2,1)}, u32[]{:S(2)}, u32[]{:S(2)}) %collective-permute-start) | collective-permute-done | bytes 8388640 | tf_op jit(solution)/shard_map/ppermute | solution.py:25
  13.6 4.6 %shard_map.37 = (f32[2,512,512]{2,1,0:T(8,128)S(1)}, bf16[2,512,1024]{2,1,0:T(8,128)(2,1)S(1)}) custom-call(s32[2,2]{1,0:T(2,128)S(1)} %broadcast_select_fusion.users.rest_0_, bf16[2,512,1024]{2,1,0:T(8,128)(2,1)S(1)} %get-tuple-element.19.rest_1_, bf16[2,2,2,512,1024]{4,3,2,1,0:T(8,128)(2,1)} %collective-permute-done.rest_2_.rest_5_, ...), custom_call_target="tpu_custom_call" | custom-call | flops 2147483648 | bytes 6291456 | tf_op jit(solution)/shard_map/pallas_call | solution.py:215
  18.2 3.3 %shard_map.38 = (f32[2,512,512]{2,1,0:T(8,128)S(1)}, bf16[2,512,1024]{2,1,0:T(8,128)(2,1)S(1)}) custom-call(s32[2,2]{1,0:T(2,128)S(1)} %broadcast_select_fusion.users.rest_0_, bf16[2,512,1024]{2,1,0:T(8,128)(2,1)S(1)} %get-tuple-element.19.rest_1_, bf16[2,512,1024]{2,1,0:T(8,128)(2,1)S(1)} %get-tuple-element.20.rest_2_, ...), custom_call_target="tpu_custom_call" | custom-call | flops 2147483648 | bytes 6291456 | tf_op jit(solution)/shard_map/pallas_call | solution.py:215
  21.6 0.4 collective-permute-start.6
  22.0 2.7 %collective-permute-start.5 = (bf16[512,256]{1,0:T(8,128)(2,1)S(1)}, bf16[512,256]{1,0:T(8,128)(2,1)S(1)}, u32[]{:S(2)}, u32[]{:S(2)}) collective-permute-start(bf16[512,256]{1,0:T(8,128)(2,1)S(1)} %pad_maximum_fusion), channel_id=1, source_target_pairs={{0,8},{2,10},{4,12},{6,14},{8,24},{10,26},{12,28},{14,30},{16,0},{... | collective-permute-start | bytes 786440 | tf_op jit(solution)/shard_map/ppermute | solution.py:275
  25.0 2.6 %collective-permute-start.3 = (bf16[512,128]{1,0:T(8,128)(2,1)S(1)}, bf16[512,128]{1,0:T(8,128)(2,1)S(1)}, u32[]{:S(2)}, u32[]{:S(2)}) collective-permute-start(bf16[512,128]{1,0:T(8,128)(2,1)S(1)} %pad_maximum_fusion.2), channel_id=1, source_target_pairs={{0,8},{2,10},{4,12},{6,14},{8,24},{10,26},{12,28},{14,30},{16,0},{... | collective-permute-start | bytes 393224 | tf_op jit(solution)/shard_map/ppermute | solution.py:275
  27.7 0.5 %collective-permute-start.4 = (bf16[512,128]{1,0:T(8,128)(2,1)S(1)}, bf16[512,128]{1,0:T(8,128)(2,1)S(1)}, u32[]{:S(2)}, u32[]{:S(2)}) collective-permute-start(bf16[512,128]{1,0:T(8,128)(2,1)S(1)} %pad_maximum_fusion.3), channel_id=1, source_target_pairs={{0,8},{2,10},{4,12},{6,14},{8,24},{10,26},{12,28},{14,30},{16,0},{... | collective-permute-start | bytes 393224 | tf_op jit(solution)/shard_map/ppermute | solution.py:275
  28.2 4.7 %collective-permute-done.5.rest_2_ = bf16[512,256]{1,0:T(8,128)(2,1)S(1)} collective-permute-done((bf16[512,256]{1,0:T(8,128)(2,1)S(1)}, bf16[512,256]{1,0:T(8,128)(2,1)S(1)}, u32[]{:S(2)}, u32[]{:S(2)}) %collective-permute-start.5) | collective-permute-done | bytes 262176 | tf_op jit(solution)/shard_map/ppermute | solution.py:275
  32.9 2.4 %shard_map.39.rest_3_ = f32[2,512,512]{2,1,0:T(8,128)S(1)} custom-call(bf16[2,512,1024]{2,1,0:T(8,128)(2,1)S(1)} %get-tuple-element.18.rest_0_, bf16[2,512,1024]{2,1,0:T(8,128)(2,1)S(1)} %get-tuple-element.22.rest_1_, bf16[512,256]{1,0:T(8,128)(2,1)S(1)} %collective-permute-done.5.rest_2_), custom_call_target="tpu_custom_call" | custom-call | flops 2147483648 | bytes 6291456 | tf_op jit(solution)/shard_map/pallas_call | solution.py:215
  35.2 2.9 %collective-permute-done.4.rest_2_ = bf16[512,128]{1,0:T(8,128)(2,1)S(1)} collective-permute-done((bf16[512,128]{1,0:T(8,128)(2,1)S(1)}, bf16[512,128]{1,0:T(8,128)(2,1)S(1)}, u32[]{:S(2)}, u32[]{:S(2)}) %collective-permute-start.4) | collective-permute-done | bytes 131104 | tf_op jit(solution)/shard_map/ppermute | solution.py:275
  38.2 1.9 %shard_map.40.sums_ref = f32[2,512,512]{2,1,0:T(8,128)S(1)} custom-call(bf16[2,512,1024]{2,1,0:T(8,128)(2,1)S(1)} %get-tuple-element.18.rest_0_, bf16[2,512,1024]{2,1,0:T(8,128)(2,1)S(1)} %get-tuple-element.22.rest_1_, bf16[512,128]{1,0:T(8,128)(2,1)S(1)} %collective-permute-done.4.rest_2_, f32[2,512,512]{2,1,0:T(8,128)S(1)} %shard_map.39.rest_3_), custom_call_target="tpu_custom_call" | custom-call | flops 1073741824 | bytes 6291456 | tf_op jit(solution)/shard_map/pallas_call | solution.py:215
  40.1 0.5 %fold.1.rest_3_.source_ref = f32[2,512,512]{2,1,0:T(8,128)S(1)} custom-call(s32[3,8,128]{2,1,0:T(8,128)S(1)} %get-tuple-element.17.slot_ref, f32[2,512,512]{2,1,0:T(8,128)S(1)} %shard_map.40.sums_ref, f32[2,512,512]{2,1,0:T(8,128)S(1)} %get-tuple-element.23.own_ref, f32[2,512,512]{2,1,0:T(8,128)S(1)} %collective-permute-done.6.other_ref), custom_call_target="tpu_custom_call" | custom-call | tf_op jit(solution)/shard_map/fold/pallas_call | solution.py:95
  40.7 1.7 %shard_map.41 = (f32[256,512]{1,0:T(8,128)S(1)}, f32[256,512]{1,0:T(8,128)S(1)}, bf16[2,512,512]{2,1,0:T(8,128)(2,1)S(1)}) custom-call(bf16[2,512,1024]{2,1,0:T(8,128)(2,1)S(1)} %get-tuple-element.18.rest_0_, bf16[2,512,1024]{2,1,0:T(8,128)(2,1)S(1)} %get-tuple-element.22.rest_1_, bf16[512,128]{1,0:T(8,128)(2,1)S(1)} %collective-permute-done.3.rest_2_, ...), custom_call_target="tpu_custom_call" | custom-call | flops 1073741824 | bytes 6291456 | tf_op jit(solution)/shard_map/pallas_call | solution.py:215
  42.4 0.5 %add_imag.1 = (f32[256,512]{1,0:T(8,128)S(1)}, f32[256,512]{1,0:T(8,128)S(1)}) custom-call(bf16[2,512,512]{2,1,0:T(8,128)(2,1)S(1)} %get-tuple-element.25.left_ref, f32[2,512,512]{2,1,0:T(8,128)S(1)} %fold.1.rest_3_.source_ref), custom_call_target="tpu_custom_call" | custom-call | flops 268435456 | bytes 2097152 | tf_op jit(solution)/shard_map/add_imag/pallas_call | solution.py:108
  42.9 0.5 %collective-permute-start.7 = (f32[256,512]{1,0:T(8,128)S(1)}, f32[256,512]{1,0:T(8,128)S(1)}, u32[]{:S(2)}, u32[]{:S(2)}) collective-permute-start(f32[256,512]{1,0:T(8,128)S(1)} %get-tuple-element.24), channel_id=1, source_target_pairs={{0,1},{1,0},{2,3},{3,2},{4,5},{5,4},{6,7},{7,6},{8,9},{9,8},{10,11... | collective-permute-start | bytes 1572872 | tf_op jit(solution)/shard_map/ppermute | solution.py:25
  43.4 1.2 %place.2.rest_0_ = f32[2,2,256,512]{3,2,1,0:T(8,128)} custom-call(s32[3,8,128]{2,1,0:T(8,128)S(1)} %get-tuple-element.17.slot_ref, f32[256,512]{1,0:T(8,128)S(1)} %get-tuple-element.27.real_ref, f32[256,512]{1,0:T(8,128)S(1)} %get-tuple-element.28.imag_ref), custom_call_target="tpu_custom_call" | custom-call | tf_op jit(solution)/shard_map/place/pallas_call | solution.py:245
  44.8 0.7 %collective-permute-done.7.real_ref = f32[256,512]{1,0:T(8,128)S(1)} collective-permute-done((f32[256,512]{1,0:T(8,128)S(1)}, f32[256,512]{1,0:T(8,128)S(1)}, u32[]{:S(2)}, u32[]{:S(2)}) %collective-permute-start.7) | collective-permute-done | bytes 524320 | tf_op jit(solution)/shard_map/ppermute | solution.py:25
  45.6 1.2 %place.3 = f32[2,2,256,512]{3,2,1,0:T(8,128)} custom-call(s32[3,8,128]{2,1,0:T(8,128)S(1)} %get-tuple-element.17.slot_ref, f32[256,512]{1,0:T(8,128)S(1)} %collective-permute-done.7.real_ref, f32[256,512]{1,0:T(8,128)S(1)} %collective-permute-done.8.imag_ref, f32[2,2,256,512]{3,2,1,0:T(8,128)} %place.2.rest_0_), custom_call_target="tpu_custom_call", output_to_operand_aliasing={{}: (3, {})} | custom-call | tf_op jit(solution)/shard_map/place/pallas_call | solution.py:245
  (19 shorter events, 1.1 us)
Async XLA Ops:
  0.0 1.2 %copy-start = (bf16[2,512,512]{2,1,0:T(8,128)(2,1)S(1)}, bf16[2,512,512]{2,1,0:T(8,128)(2,1)}, u32[]{:S(2)}) copy-start(bf16[2,512,512]{2,1,0:T(8,128)(2,1)} %param.4) | copy-start | bytes 3145732
  0.0 7.2 %copy-start.1 = (s32[2,32]{1,0:T(2,128)S(1)}, s32[2,32]{1,0:T(2,128)}, u32[]{:S(2)}) copy-start(s32[2,32]{1,0:T(2,128)} %param.5) | copy-start | bytes 772
  0.0 13.6 %collective-permute-start = (bf16[2,2,2,512,1024]{4,3,2,1,0:T(8,128)(2,1)}, bf16[2,2,2,512,1024]{4,3,2,1,0:T(8,128)(2,1)}, u32[]{:S(2)}, u32[]{:S(2)}) collective-permute-start(bf16[2,2,2,512,1024]{4,3,2,1,0:T(8,128)(2,1)} %pair_ref.1), channel_id=1, source_target_pairs={{0,1},{1,0},{2,3},{3,2},{4,5},{5,4},{6,7},{7,6},{8,9},{9,8},{10,11... | collective-permute-start | bytes 25165832 | tf_op jit(solution)/shard_map/ppermute | solution.py:25
  1.4 10.8 %collective-permute-start.1 = (bf16[512,256]{1,0:T(8,128)(2,1)S(1)}, bf16[512,256]{1,0:T(8,128)(2,1)S(1)}, u32[]{:S(2)}, u32[]{:S(2)}) collective-permute-start(bf16[512,256]{1,0:T(8,128)(2,1)S(1)} %pad_maximum_fusion), channel_id=1, source_target_pairs={{0,16},{2,18},{4,20},{6,22},{8,0},{10,2},{12,4},{14,6},{16,24},{18... | collective-permute-start | bytes 786440 | tf_op jit(solution)/shard_map/ppermute | solution.py:275
  5.6 12.7 %collective-permute-start.2 = (bf16[512,256]{1,0:T(8,128)(2,1)S(1)}, bf16[512,256]{1,0:T(8,128)(2,1)S(1)}, u32[]{:S(2)}, u32[]{:S(2)}) collective-permute-start(bf16[512,256]{1,0:T(8,128)(2,1)S(1)} %pad_maximum_fusion.1), channel_id=1, source_target_pairs={{0,16},{2,18},{4,20},{6,22},{8,0},{10,2},{12,4},{14,6},{16,24},{18... | collective-permute-start | bytes 786440 | tf_op jit(solution)/shard_map/ppermute | solution.py:275
  21.6 18.6 %collective-permute-start.6 = (f32[2,512,512]{2,1,0:T(8,128)S(1)}, f32[2,512,512]{2,1,0:T(8,128)S(1)}, u32[]{:S(2)}, u32[]{:S(2)}) collective-permute-start(f32[2,512,512]{2,1,0:T(8,128)S(1)} %get-tuple-element.23.own_ref), channel_id=1, source_target_pairs={{0,1},{1,0},{2,3},{3,2},{4,5},{5,4},{6,7},{7,6},{8,9},{9,8},{10,11... | collective-permute-start | bytes 6291464 | tf_op jit(solution)/shard_map/ppermute | solution.py:25
  22.0 10.9 %collective-permute-start.5 = (bf16[512,256]{1,0:T(8,128)(2,1)S(1)}, bf16[512,256]{1,0:T(8,128)(2,1)S(1)}, u32[]{:S(2)}, u32[]{:S(2)}) collective-permute-start(bf16[512,256]{1,0:T(8,128)(2,1)S(1)} %pad_maximum_fusion), channel_id=1, source_target_pairs={{0,8},{2,10},{4,12},{6,14},{8,24},{10,26},{12,28},{14,30},{16,0},{... | collective-permute-start | bytes 786440 | tf_op jit(solution)/shard_map/ppermute | solution.py:275
  25.0 15.7 %collective-permute-start.3 = (bf16[512,128]{1,0:T(8,128)(2,1)S(1)}, bf16[512,128]{1,0:T(8,128)(2,1)S(1)}, u32[]{:S(2)}, u32[]{:S(2)}) collective-permute-start(bf16[512,128]{1,0:T(8,128)(2,1)S(1)} %pad_maximum_fusion.2), channel_id=1, source_target_pairs={{0,8},{2,10},{4,12},{6,14},{8,24},{10,26},{12,28},{14,30},{16,0},{... | collective-permute-start | bytes 393224 | tf_op jit(solution)/shard_map/ppermute | solution.py:275
  27.7 10.5 %collective-permute-start.4 = (bf16[512,128]{1,0:T(8,128)(2,1)S(1)}, bf16[512,128]{1,0:T(8,128)(2,1)S(1)}, u32[]{:S(2)}, u32[]{:S(2)}) collective-permute-start(bf16[512,128]{1,0:T(8,128)(2,1)S(1)} %pad_maximum_fusion.3), channel_id=1, source_target_pairs={{0,8},{2,10},{4,12},{6,14},{8,24},{10,26},{12,28},{14,30},{16,0},{... | collective-permute-start | bytes 393224 | tf_op jit(solution)/shard_map/ppermute | solution.py:275
  42.9 2.0 %collective-permute-start.8 = (f32[256,512]{1,0:T(8,128)S(1)}, f32[256,512]{1,0:T(8,128)S(1)}, u32[]{:S(2)}, u32[]{:S(2)}) collective-permute-start(f32[256,512]{1,0:T(8,128)S(1)} %get-tuple-element.26), channel_id=1, source_target_pairs={{0,1},{1,0},{2,3},{3,2},{4,5},{5,4},{6,7},{7,6},{8,9},{9,8},{10,11... | collective-permute-start | bytes 1572872 | tf_op jit(solution)/shard_map/ppermute | solution.py:25
  42.9 2.6 %collective-permute-start.7 = (f32[256,512]{1,0:T(8,128)S(1)}, f32[256,512]{1,0:T(8,128)S(1)}, u32[]{:S(2)}, u32[]{:S(2)}) collective-permute-start(f32[256,512]{1,0:T(8,128)S(1)} %get-tuple-element.24), channel_id=1, source_target_pairs={{0,1},{1,0},{2,3},{3,2},{4,5},{5,4},{6,7},{7,6},{8,9},{9,8},{10,11... | collective-permute-start | bytes 1572872 | tf_op jit(solution)/shard_map/ppermute | solution.py:25
